TPU v7x, 32 devices: a whole 2x2x4 slice. The times are simulated.
32 devices in a mesh: zero: 8 (over y, x, core), width: 4 (over z).
Axes of the slice: x: 2, y: 2, z: 4, core: 2. Of those that a mesh axis runs over, the one named last changes fastest.
Arguments:
- train_query: bfloat16 [3584, 4096], P('zero', 'width'), may hold values from -0.09375 to 0.09375
- low_query: bfloat16 [3584, 32], P('zero'), may hold values from -0.09375 to 0.09375
- high_query: bfloat16 [32, 4096], P(None, 'width'), may hold values from -1 to 1
- train_key: bfloat16 [3584, 2048], P('zero', 'width'), may hold values from -0.09375 to 0.09375
- low_key: bfloat16 [3584, 32], P('zero'), may hold values from -0.09375 to 0.09375
- high_key: bfloat16 [32, 2048], P(None, 'width'), may hold values from -1 to 1
- train_value: bfloat16 [3584, 2048], P('zero', 'width'), may hold values from -0.09375 to 0.09375
- low_value: bfloat16 [3584, 32], P('zero'), may hold values from -0.09375 to 0.09375
- high_value: bfloat16 [32, 2048], P(None, 'width'), may hold values from -1 to 1
- train_mixed: bfloat16 [4096, 3584], P('width', 'zero'), may hold values from -0.09375 to 0.09375
- low_mixed: bfloat16 [4096, 32], P('width'), may hold values from -0.09375 to 0.09375
- high_mixed: bfloat16 [32, 3584], P(None, 'zero'), may hold values from -1 to 1
- norm_train: float32 [3584], P(('zero', 'width')), may hold values from 0.25 to 1.75
- norm_step: float32 [3584], P(('zero', 'width')), may hold values from -0.3 to 0.3
Outputs:
- ready_query: bfloat16 [4096, 3584], P('width')
- ready_key: bfloat16 [2048, 3584], P('width')
- ready_value: bfloat16 [2048, 3584], P('width')
- ready_mixed: bfloat16 [3584, 4096], P(None, 'width')
- serve_norm: bfloat16 [3584], replicated
All inputs are finite; a program needn't handle non-finite values.
Results may differ from a plain program's by a relative error of at most 0.001.
Values may be sent and summed in bfloat16 or wider, within the bound.
A program may use at most 128 MiB of HBM per device.

v0:
```python
import functools
import math

import jax
import jax.numpy as jnp
from jax import lax
from jax.experimental import pallas as pl
from jax.experimental.pallas import tpu as pltpu
from jax.sharding import PartitionSpec as P

mix_rate = 0.5
CORES = 2
LANES = 128
F32 = jnp.float32
BF16 = jnp.bfloat16
SPLIT = 4
VMEM_BYTES = 67_043_328
PLACE = pltpu.VMEM
GATHERED = pltpu.VMEM


def plain_body(
    train_query, low_query, high_query, train_key, low_key, high_key, train_value, low_value, high_value,
    train_mixed, low_mixed, high_mixed, norm_train, norm_step,
):
    def merged(train, low, high):
        return (train.astype(F32) + mix_rate * jnp.dot(low, high, preferred_element_type=F32)).astype(BF16)

    return (
        lax.all_gather(merged(train_query, low_query, high_query), "zero", axis=0, tiled=True).T,
        lax.all_gather(merged(train_key, low_key, high_key), "zero", axis=0, tiled=True).T,
        lax.all_gather(merged(train_value, low_value, high_value), "zero", axis=0, tiled=True).T,
        lax.all_gather(merged(train_mixed, low_mixed, high_mixed).T, "zero", axis=0, tiled=True),
        lax.all_gather((norm_train + norm_step).astype(BF16), ("zero", "width"), axis=0, tiled=True),
    )


def kernel(
    zeros, widths,
    tq_h, lq_h, hq_h, tk_h, lk_h, hk_h, tv_h, lv_h, hv_h, tm_h, lm_h, hm_h, nt_h, ns_h,
    oq, ok, ov, om, norm_out,
    lq, hq, lk, hk, lv, hv, tm, lm, hm, nt, ns, fetched, on, own_q, own_k, own_v, own_m, pq, pk, pv, plq, plk, plv, keep, swap_send, swap_recv, send, recv, nsend, nrecv,
):
    me, w = lax.axis_index("zero"), lax.axis_index("width")
    c = lax.rem(me, 2)
    x = lax.rem(lax.div(me, 2), 2)
    y = lax.div(me, 4)
    chip = lax.div(me, 2)
    partner, xn, yn = me + 1 - 2 * c, me + 2 - 4 * x, me + 4 - 8 * y
    chip_x, chip_y, chip_d = chip + 1 - 2 * x, chip + 2 - 4 * y, 3 - chip
    rows = tq_h.shape[0]
    pair = 2 * rows

    def rank_dot(left, right):
        return lax.dot_general(left, right, (((0,), (0,)), ((), ())), preferred_element_type=F32)

    def remote(src, dst, ssem, rsem, **where):
        return pltpu.make_async_remote_copy(
            src_ref=src, dst_ref=dst, send_sem=ssem, recv_sem=rsem,
            device_id=where, device_id_type=pl.DeviceIdType.MESH,
        )

    fetches = []
    for k, (src, dst) in enumerate((
        (nt_h, nt), (ns_h, ns), (lm_h, lm), (hm_h, hm), (tm_h, tm), (tq_h, pq), (lq_h, lq.at[c]), (hq_h, hq),
        (tk_h, pk), (lk_h, lk.at[c]), (hk_h, hk), (tv_h, pv), (lv_h, lv.at[c]), (hv_h, hv),
    )):
        if k in (5, 8, 11):
            half = src.shape[1] // 2
            cols = pl.ds(pl.multiple_of(c * half, LANES), half)
            dst = dst.at[pl.ds(pl.multiple_of(rows * c, 16), rows), :]
            src = src.at[:, cols]
        copy = pltpu.make_async_copy(src, dst, fetched.at[k])
        copy.start()
        fetches.append(copy)

    others = [lax.rem(me + d, zeros) for d in range(1, zeros)]
    barrier = pltpu.get_barrier_semaphore()
    for other in others:
        pl.semaphore_signal(barrier, inc=1, device_id={"zero": other}, device_id_type=pl.DeviceIdType.MESH)
    for d in range(1, widths):
        pl.semaphore_signal(
            barrier, inc=1, device_id={"width": lax.rem(w + d, widths)}, device_id_type=pl.DeviceIdType.MESH
        )

    for copy in fetches[2:5]:
        copy.wait()
    step = 2 * LANES
    for i in range(tm.shape[1] // step):
        at = slice(i * step, (i + 1) * step)
        merged = tm[:, at].astype(F32) + mix_rate * rank_dot(hm[...], lm[:, at])
        own_m[:, at] = merged.astype(BF16)
    pl.semaphore_wait(barrier, zeros + widths - 2)
    kept = [pltpu.make_async_copy(own_m, om.at[pl.ds(pl.multiple_of(rows * me, 16), rows), :], keep.at[3])]
    kept[0].start()

    part = rows // 2

    def mixed_item(h):
        return lambda p, cc: om.at[pl.ds(pl.multiple_of(rows * (2 * p + cc) + h * part, 16), part), :]

    def item(out, start, size, share):
        return lambda p, cc: out.at[
            pl.ds(pl.multiple_of(share * cc + start, 16), size), pl.ds(pl.multiple_of(pair * p, LANES), pair)
        ]

    nq, nk = oq.shape[0] // 2, ok.shape[0] // 2
    last = nk // 4
    first = [mixed_item(0), item(oq, 0, nq // 2, nq), item(ok, 0, nk - last, nk), item(ok, nk - last, last, nk)]
    second = [mixed_item(1), item(oq, nq // 2, nq // 2, nq), item(ov, 0, nk - last, nk), item(ov, nk - last, last, nk)]
    items = first + second
    sources = [
        own_m.at[:part, :], own_q.at[: nq // 2, :], own_k.at[: nk - last, :], own_k.at[nk - last :, :],
        own_m.at[part:, :], own_q.at[nq // 2 :, :], own_v.at[: nk - last, :], own_v.at[nk - last :, :],
    ]
    n = len(first)
    TO_X, TO_Y, ON, P_OWN, P_X, P_Y, P_D = range(7)
    copies = {}

    def go(k, kind, p, where):
        region = items[k](p, c)
        source = sources[k] if kind in (TO_X, TO_Y, P_OWN) else region
        copy = remote(source, region, send.at[k, kind], recv.at[k, kind], zero=where)
        copy.start()
        copies[k, kind] = copy

    def own(j):
        go(j, TO_X, chip, xn)
        go(n + j, TO_Y, chip, yn)

    own(0)

    mine = pl.ds(pl.multiple_of(rows * c, 16), rows)
    swaps = []
    for k, (train, low, held, held_low) in enumerate(((tq_h, lq_h, pq, lq), (tk_h, lk_h, pk, lk), (tv_h, lv_h, pv, lv))):
        half = train.shape[1] // 2
        cols = pl.ds(pl.multiple_of((1 - c) * half, LANES), half)
        for e, (src, dst) in enumerate(((train.at[:, cols], held.at[mine, :]), (low, held_low.at[c]))):
            copy = remote(src, dst, swap_send.at[2 * k + e], swap_recv.at[2 * k + e], zero=partner)
            copy.start()
            swaps.append(copy)

    for copy in fetches[:2]:
        copy.wait()
    on[me, w] = jnp.pad(nt[...] + ns[...], ((0, 0), (0, LANES - nt.shape[1])))
    small = []
    for d in range(1, widths):
        copy = remote(
            on.at[me, w], on.at[me, w], nsend.at[d - 1], nrecv.at[d - 1], width=lax.rem(w + d, widths)
        )
        copy.start()
        small.append(copy)

    def merge(e, out, own_out, held, low, held_low, high):
        half = held.shape[1]
        held_low[:, :rows] = low[0]
        held_low[:, rows:] = low[1]
        cols = pl.ds(pl.multiple_of(c * half, LANES), half)
        for j in range(pair // LANES):
            at = slice(j * LANES, (j + 1) * LANES)
            merged = held[at, :].astype(F32) + mix_rate * rank_dot(held_low[:, at], high[:, cols])
            own_out[:, at] = merged.T.astype(BF16)
        here = out.at[
            pl.ds(pl.multiple_of(c * half, 16), half), pl.ds(pl.multiple_of(pair * chip, LANES), pair)
        ]
        kept.append(pltpu.make_async_copy(own_out, here, keep.at[e]))
        kept[-1].start()

    for copy in fetches[5:] + swaps:
        copy.wait()
    merge(0, oq, own_q, pq, lq, plq, hq)
    own(1)
    for copy in small:
        copy.wait()
    for d in range(1, zeros):
        copy = remote(
            on.at[me], on.at[me], nsend.at[widths - 2 + d], nrecv.at[widths - 2 + d], zero=others[d - 1]
        )
        copy.start()
        small.append(copy)
    merge(1, ok, own_k, pk, lk, plk, hk)
    merge(2, ov, own_v, pv, lv, plv, hv)
    own(2)
    own(3)
    for j in range(n):
        go(n + j, TO_X, chip, xn)
        go(j, TO_Y, chip, yn)
    for k in range(2 * n):
        go(k, P_OWN, chip, partner)

    for j in range(n):
        copies[j, TO_X].wait_recv()
        go(j, ON, chip_x, yn)
        go(j, P_X, chip_x, partner)
        copies[n + j, TO_Y].wait_recv()
        go(n + j, ON, chip_y, xn)
        go(n + j, P_Y, chip_y, partner)
    for j in range(n):
        copies[n + j, TO_X].wait_recv()
        go(n + j, P_X, chip_x, partner)
        copies[j, TO_Y].wait_recv()
        go(j, P_Y, chip_y, partner)
    for j in range(n):
        for k in (j, n + j):
            copies[k, ON].wait_recv()
            go(k, P_D, chip_d, partner)
    for copy in kept:
        copy.wait()
    for copy in small[widths - 1 :]:
        copy.wait()
    norm_out[...] = on[...]
    for (k, kind), copy in copies.items():
        copy.wait_send()
        if kind >= P_OWN:
            copy.wait_recv()


def publish(*refs):
    n = len(refs) // 2
    done = refs[-1]
    copies = []
    for k, (src, dst) in enumerate(zip(refs[:n], refs[n : 2 * n])):
        size = src.shape[0] // SPLIT
        for e in range(SPLIT):
            at = pl.ds(e * size, size)
            copies.append(pltpu.make_async_copy(src.at[at, :], dst.at[at, :], done.at[k, e]))
            copies[-1].start()
    for copy in copies:
        copy.wait()


def fast_body(zeros, widths, *args):
    tq, lq, hq, tk, lk, hk, tv, lv, hv, tm, lm, hm, nt, ns = args
    rows, depth = tq.shape[0], tq.shape[0] * zeros
    VM, HBM = pltpu.VMEM, pltpu.MemorySpace.HBM
    new = jax.ShapeDtypeStruct
    shapes = [(tq.shape[1], depth), (tk.shape[1], depth), (tv.shape[1], depth), (depth, tm.shape[0])]
    pair = 2 * rows
    held = 2 * sum(a * b for a, b in shapes)
    dma = pltpu.SemaphoreType.DMA
    small = widths - 1 + zeros - 1
    moved = [tq, lq.T, hq, tk, lk.T, hk, tv, lv.T, hv, tm.T, lm.T, hm, nt[None, :], ns[None, :]]
    local = [VM(((2,) if i in (1, 4, 7) else ()) + a.shape, a.dtype) for i, a in enumerate(moved) if i not in (0, 3, 6)]
    *full, on = pl.pallas_call(
        functools.partial(kernel, zeros, widths),
        out_shape=[GATHERED(s, BF16) for s in shapes] + [new((zeros, widths, 1, LANES), F32)],
        in_specs=[pl.BlockSpec(memory_space=HBM)] * len(args),
        out_specs=[pl.BlockSpec(memory_space=PLACE)] * len(shapes) + [pl.BlockSpec(memory_space=VM)],
        scratch_shapes=local + [
            dma((len(args),)), VM((zeros, widths, 1, LANES), F32),
            VM((tq.shape[1] // 2, pair), BF16), VM((tk.shape[1] // 2, pair), BF16), VM((tv.shape[1] // 2, pair), BF16),
            VM((tm.shape[1], tm.shape[0]), BF16),
            VM((pair, tq.shape[1] // 2), BF16), VM((pair, tk.shape[1] // 2), BF16), VM((pair, tv.shape[1] // 2), BF16),
            VM((lq.shape[1], pair), BF16), VM((lk.shape[1], pair), BF16), VM((lv.shape[1], pair), BF16),
            dma((4,)), dma((6,)), dma((6,)), dma((8, 7)), dma((8, 7)), dma((small,)), dma((small,)),
        ],
        compiler_params=pltpu.CompilerParams(
            collective_id=0, has_side_effects=True, vmem_limit_bytes=VMEM_BYTES - held - 48 * 1024
        ),
        name="gather_merged",
    )(*moved)
    norm = on[:, :, 0, : nt.shape[0]].reshape(-1).astype(BF16)
    full = pl.pallas_call(
        publish,
        out_shape=[new(s, BF16) for s in shapes],
        in_specs=[pl.BlockSpec(memory_space=PLACE)] * len(shapes),
        out_specs=[pl.BlockSpec(memory_space=HBM)] * len(shapes),
        scratch_shapes=[dma((len(shapes), SPLIT))],
        compiler_params=pltpu.CompilerParams(vmem_limit_bytes=2**20),
        name="publish",
    )(*full)
    return (*full, norm)


def solution(mesh):
    placed = (
        P("zero", "width"), P("zero", None), P(None, "width"),
        P("zero", "width"), P("zero", None), P(None, "width"),
        P("zero", "width"), P("zero", None), P(None, "width"),
        P("width", "zero"), P("width", None), P(None, "zero"),
        P(("zero", "width")), P(("zero", "width")),
    )
    zeros, widths = mesh.shape["zero"], mesh.shape["width"]
    side = math.isqrt(zeros // CORES)

    def body(*args):
        rows = args[0].shape[0]
        square = side == 2 and CORES * side * side == zeros
        if square and CORES * rows % LANES == 0 and rows % 32 == 0:
            return fast_body(zeros, widths, *args)
        return plain_body(*args)

    return jax.shard_map(
        body,
        mesh=mesh,
        in_specs=placed,
        out_specs=(P("width", None), P("width", None), P("width", None), P(None, "width"), P()),
        check_vma=False,
    )
```

profile of v0, /device:TPU:0, one launch (start us, length us, event | category | flops | bytes accessed | tf_op | source)
XLA Modules:
  0.0 108.2 jit_solution(11547409781236263284)
XLA Ops:
  0.6 99.2 %gather_merged.1 = (bf16[1024,3584]{1,0:T(8,128)(2,1)S(1)}, bf16[512,3584]{1,0:T(8,128)(2,1)S(1)}, bf16[512,3584]{1,0:T(8,128)(2,1)S(1)}, bf16[3584,1024]{1,0:T(8,128)(2,1)S(1)}, f32[8,4,1,128]{3,2,1,0:T(1,128)}) custom-call(bf16[448,1024]{1,0:T(8,128)(2,1)} %tq_h.1, bf16[32,448]{1,0:T(8,128)(2,1)} %bitcast.9, bf16[32,1024]{1,0:T(8,128)(2,1)} %hq_h.1, ...), custom_call_target="tpu_custom_call" | custom-call | tf_op jit(solution)/shard_map/gather_merged/pallas_call | solution.py:244
  99.9 0.0 copy-start
  99.9 7.6 %publish.1 = (bf16[1024,3584]{1,0:T(8,128)(2,1)}, bf16[512,3584]{1,0:T(8,128)(2,1)}, bf16[512,3584]{1,0:T(8,128)(2,1)}, bf16[3584,1024]{1,0:T(8,128)(2,1)}) custom-call(bf16[1024,3584]{1,0:T(8,128)(2,1)S(1)} %get-tuple-element.14.refs_0_, bf16[512,3584]{1,0:T(8,128)(2,1)S(1)} %get-tuple-element.15.refs_1_, bf16[512,3584]{1,0:T(8,128)(2,1)S(1)} %get-tuple-element.16.refs_2_, ...), custom_call_target="tpu_custom_call" | custom-call | tf_op jit(solution)/shard_map/publish/pallas_call | solution.py:263
  107.5 0.0 copy-done
  107.5 0.1 fusion
  107.5 0.7 convert_element_type.4
Async XLA Ops:
  99.9 7.6 %copy-start = (f32[8,4,1,128]{3,2,1,0:T(1,128)S(1)}, f32[8,4,1,128]{3,2,1,0:T(1,128)}, u32[]{:S(2)}) copy-start(f32[8,4,1,128]{3,2,1,0:T(1,128)} %get-tuple-element.22) | copy-start | bytes 49156
where the time goes:
time: 108 us
  Pallas kernels  107 us (99%)
    pallas_call x1, Pallas kernels, fast_body(): pl.pallas_call(functools.partial(kernel, zeros, widths), out_shape=[GATHE...  99.2 us
    pallas_call x1, Pallas kernels, fast_body(): pl.pallas_call(publish, out_shape=[new(s, BF16) for s in shapes], in_spec...  7.6 us

commit v1 on v0

v1 whole, which is shorter than its diff:
```python
import functools
import math

import jax
import jax.numpy as jnp
from jax import lax
from jax.experimental import pallas as pl
from jax.experimental.pallas import tpu as pltpu
from jax.sharding import PartitionSpec as P

mix_rate = 0.5
CORES = 2
LANES = 128
F32 = jnp.float32
BF16 = jnp.bfloat16
EARLY = 5
VMEM_BYTES = 67_043_328
VMEM = pltpu.VMEM
HBM = pltpu.MemorySpace.HBM
TO_X, TO_Y, ON, P_OWN, P_X, P_Y = range(6)


def plain_body(
    train_query, low_query, high_query, train_key, low_key, high_key, train_value, low_value, high_value,
    train_mixed, low_mixed, high_mixed, norm_train, norm_step,
):
    def merged(train, low, high):
        return (train.astype(F32) + mix_rate * jnp.dot(low, high, preferred_element_type=F32)).astype(BF16)

    return (
        lax.all_gather(merged(train_query, low_query, high_query), "zero", axis=0, tiled=True).T,
        lax.all_gather(merged(train_key, low_key, high_key), "zero", axis=0, tiled=True).T,
        lax.all_gather(merged(train_value, low_value, high_value), "zero", axis=0, tiled=True).T,
        lax.all_gather(merged(train_mixed, low_mixed, high_mixed).T, "zero", axis=0, tiled=True),
        lax.all_gather((norm_train + norm_step).astype(BF16), ("zero", "width"), axis=0, tiled=True),
    )


class Place:
    def __init__(self):
        self.me, self.w = lax.axis_index("zero"), lax.axis_index("width")
        me = self.me
        self.c = lax.rem(me, 2)
        x = lax.rem(lax.div(me, 2), 2)
        self.y = lax.div(me, 4)
        self.chip = lax.div(me, 2)
        self.partner, self.xn, self.yn = me + 1 - 2 * self.c, me + 2 - 4 * x, me + 4 - 8 * self.y
        self.chip_x, self.chip_y, self.chip_d = self.chip + 1 - 2 * x, self.chip + 2 - 4 * self.y, 3 - self.chip


def remote(src, dst, ssem, rsem, **where):
    return pltpu.make_async_remote_copy(
        src_ref=src, dst_ref=dst, send_sem=ssem, recv_sem=rsem, device_id=where, device_id_type=pl.DeviceIdType.MESH
    )


def tell(sem, **where):
    pl.semaphore_signal(sem, inc=1, device_id=where, device_id_type=pl.DeviceIdType.MESH)


def unit_list(rows, mix, nq, nk):
    quarter = mix // 4
    parts = ((0, nk // 2), (nk // 2, nk // 4), (nk - nk // 4, nk // 4))
    first = [(3, 0, quarter), (3, quarter, quarter), (0, 0, nq // 4), (0, nq // 4, nq // 4)]
    second = [(3, 2 * quarter, quarter), (3, 3 * quarter, quarter), (0, nq // 2, nq // 4), (0, 3 * nq // 4, nq // 4)]
    return first + [(1, *p) for p in parts] + second + [(2, *p) for p in parts]


def region(unit, outs, rows, chip, c):
    a, start, size = unit
    out = outs[a]
    if a == 3:
        return out.at[pl.ds(pl.multiple_of(rows * (2 * chip + c), 16), rows), start : start + size]
    pair = 2 * rows
    return out.at[
        pl.ds(pl.multiple_of(c * (out.shape[0] // 2) + start, 16), size), pl.ds(pl.multiple_of(pair * chip, LANES), pair)
    ]


def arrived(ref, sem):
    pltpu.make_async_copy(ref, ref, sem).wait()


def gather(
    zeros, widths,
    tq_h, lq_h, hq_h, tk_h, lk_h, hk_h, tv_h, lv_h, hv_h, tm_h, lm_h, hm_h, nt_h, ns_h,
    oq, ok, ov, om, on,
    tm, pair_m, held, lows, highs, gains, own_q, own_k, own_v, own_m, joined,
    fetched, keep, swap_send, swap_recv, send, arrive, across, early_send, early_recv, nsend, nrecv,
):
    at = Place()
    c, chip = at.c, at.chip
    rows = tq_h.shape[0]
    pair = 2 * rows
    mix = tm_h.shape[1]
    quarter = mix // 4
    outs = (oq, ok, ov, om)
    nq, nk = oq.shape[0] // 2, ok.shape[0] // 2
    units = unit_list(rows, mix, nq, nk)
    n = len(units) // 2
    share = om.at[: rows * (mix + 2 * nq + 4 * nk) // mix, :]
    LOW_HIGH, FIRST, OTHERS, GAINS, LOWS, HIGHS, TRAINS = range(7)

    def rank_dot(left, right):
        return lax.dot_general(left, right, (((0,), (0,)), ((), ())), preferred_element_type=F32)

    def fetch(src, dst, sem):
        pltpu.make_async_copy(src, dst, fetched.at[sem]).start()

    fetch(lm_h, pair_m.at[:, :mix], LOW_HIGH)
    fetch(hm_h, pair_m.at[:, mix:], LOW_HIGH)
    fetch(tm_h.at[:, :quarter], tm.at[:, :quarter], FIRST)
    barrier = pltpu.get_barrier_semaphore()
    for other in (at.xn, at.yn, at.partner):
        tell(barrier, zero=other)
    fetch(tm_h.at[:, quarter:], tm.at[:, quarter:], OTHERS)
    fetch(nt_h, gains.at[0], GAINS)
    fetch(ns_h, gains.at[1], GAINS)

    mine = pl.ds(pl.multiple_of(rows * c, 16), rows)
    spans, spot = [], 0
    for train in (tq_h, tk_h, tv_h):
        spans.append(slice(spot, spot + train.shape[1] // 2))
        spot += train.shape[1] // 2
    for k, (train, low, high) in enumerate(((tq_h, lq_h, hq_h), (tk_h, lk_h, hk_h), (tv_h, lv_h, hv_h))):
        half = train.shape[1] // 2
        cols = pl.ds(pl.multiple_of(c * half, LANES), half)
        fetch(train.at[:, cols], held.at[mine, spans[k]], TRAINS)
        fetch(low, lows.at[k, c], LOWS)
        fetch(high, highs.at[:, 2 * spans[k].start : 2 * spans[k].stop], HIGHS)

    def merge_mixed(h):
        cols = slice(h * quarter, (h + 1) * quarter)
        merged = tm[:, cols].astype(F32) + mix_rate * rank_dot(pair_m[:, mix:], pair_m[:, cols])
        own_m[:, cols] = merged.astype(BF16)

    sources = [
        own_m.at[:, s : s + size] if a == 3 else (own_q, own_k, own_v)[a].at[s : s + size, :] for a, s, size in units
    ]

    def move(k, kind):
        p = {ON: at.chip_x if k < n else at.chip_y, P_X: at.chip_x, P_Y: at.chip_y}.get(kind, chip)
        there = region(units[k], outs, rows, p, c)
        where = {TO_X: at.xn, TO_Y: at.yn, ON: at.yn if k < n else at.xn}.get(kind, at.partner)
        if kind in (TO_X, TO_Y):
            recv = arrive.at[k % n + (n if (kind == TO_X) == (k >= n) else 0)]
        elif kind == ON:
            recv = early_recv
        else:
            recv = across.at[kind - P_OWN]
        return remote(
            sources[k] if kind in (TO_X, TO_Y, P_OWN) else there, there,
            early_send if kind == ON else send.at[kind - (kind > ON)], recv, zero=where,
        )

    def come(j, late):
        a, _, size = units[j]
        both = om.at[:rows, : 2 * size] if a == 3 else oq.at[: 2 * size, :pair]
        arrived(both, arrive.at[j + n * late])

    arrived(pair_m, fetched.at[LOW_HIGH])
    arrived(tm.at[:, :quarter], fetched.at[FIRST])
    merge_mixed(0)
    pl.semaphore_wait(barrier, 3)
    move(0, TO_X).start()
    move(0, TO_Y).start()
    arrived(tm.at[:, quarter:], fetched.at[OTHERS])
    merge_mixed(2)
    merge_mixed(1)
    merge_mixed(3)
    move(n, TO_Y).start()
    for j in (1,):
        move(j, TO_X).start()
        move(n + j, TO_Y).start()

    for k, (train, low) in enumerate(((tq_h, lq_h), (tk_h, lk_h), (tv_h, lv_h))):
        half = train.shape[1] // 2
        cols = pl.ds(pl.multiple_of((1 - c) * half, LANES), half)
        remote(train.at[:, cols], held.at[mine, spans[k]], swap_send.at[0], swap_recv.at[0], zero=at.partner).start()
        remote(low, lows.at[k, c], swap_send.at[1], swap_recv.at[1], zero=at.partner).start()

    def keep_own(source, there):
        pltpu.make_async_copy(source, there, keep).start()

    keep_own(own_m, om.at[pl.ds(pl.multiple_of(rows * at.me, 16), rows), :])

    arrived(gains, fetched.at[GAINS])
    on[c, chip] = jnp.pad(gains[0] + gains[1], ((0, 0), (0, LANES - gains.shape[2])))
    row = on.at[c, pl.ds(chip, 1)]
    both_rows = on.at[c, pl.ds(2 * at.y, 2)]
    small = [remote(row, row, nsend.at[0], nrecv.at[0], zero=at.xn)]
    small[0].start()

    def merge(e, out, own_out):
        span = spans[e]
        half = span.stop - span.start
        joined[:, :rows] = lows[e, 0]
        joined[:, rows:] = lows[e, 1]
        cols = pl.ds(pl.multiple_of(2 * span.start + c * half, LANES), half)
        for j in range(pair // LANES):
            part = slice(j * LANES, (j + 1) * LANES)
            merged = held[part, span].astype(F32) + mix_rate * rank_dot(joined[:, part], highs[:, cols])
            own_out[:, part] = merged.T.astype(BF16)
        keep_own(own_out, out.at[
            pl.ds(pl.multiple_of(c * half, 16), half), pl.ds(pl.multiple_of(pair * chip, LANES), pair)
        ])

    theirs = pl.ds(pl.multiple_of(rows * (1 - c), 16), rows)
    arrived(lows.at[:, 0], fetched.at[LOWS])
    arrived(highs, fetched.at[HIGHS])
    arrived(held.at[mine, :], fetched.at[TRAINS])
    arrived(lows.at[:, 0], swap_recv.at[1])
    arrived(held.at[theirs, :], swap_recv.at[0])
    merge(0, oq, own_q)
    for j in (2, 3):
        move(j, TO_X).start()
        move(n + j, TO_Y).start()
    merge(1, ok, own_k)
    merge(2, ov, own_v)
    for j in range(4, n):
        move(j, TO_X).start()
        move(n + j, TO_Y).start()
    small[0].wait()
    small.append(remote(both_rows, both_rows, nsend.at[1], nrecv.at[1], zero=at.yn))
    small[1].start()
    for j in range(n):
        move(n + j, TO_X).start()
        if j > 0:
            move(j, TO_Y).start()
    for k in range(2 * n):
        move(k, P_OWN).start()

    for j in range(n):
        come(j, 0)
        if j < EARLY:
            @pl.when(c == 1)
            def _():
                move(j, ON).start()
                move(n + j, ON).start()
        move(j, P_X).start()
        move(n + j, P_Y).start()
    small[1].wait()
    small.append(remote(on.at[c], on.at[c], nsend.at[2], nrecv.at[2], zero=at.partner))
    small[2].start()
    arrived(lows.at[:, 0], swap_send.at[1])
    arrived(held.at[mine, :], swap_send.at[0])
    arrived(share, keep)
    small[2].wait()
    for j in range(n):
        come(j, 1)
        move(n + j, P_X).start()
        move(j, P_Y).start()
    for kind in range(5):
        arrived(share, send.at[kind])
    for kind in range(3):
        arrived(share, across.at[kind])

    @pl.when(c == 1)
    def _():
        early = oq.at[: early_rows(units, rows, EARLY), :]
        arrived(early, early_send)
        arrived(early, early_recv)


def early_rows(units, rows, count):
    return 2 * sum(size * rows if a == 3 else size * 2 * rows for a, _, size in units[:count]) // (8 * rows)


def finish(zeros, widths, *refs):
    (
        _, oq, ok, ov, om, on, dq, dk, dv, dm, norm, every, flat,
        ready, copied, on_send, on_recv, send, recv, nsend, nrecv, psend, precv,
    ) = refs
    at = Place()
    c = at.c
    outs, diag = (oq, ok, ov, om), (dq, dk, dv, dm)
    rows = dm.shape[0] // 2
    mix, nq, nk = om.shape[1], oq.shape[0] // 2, ok.shape[0] // 2
    units = unit_list(rows, mix, nq, nk)
    n = len(units) // 2
    share = om.at[: rows * (mix + 2 * nq + 4 * nk) // mix, :]

    barrier = pltpu.get_barrier_semaphore()
    for other in (at.xn, at.yn):
        tell(barrier, zero=other)

    @pl.when(c == 0)
    def _():
        tell(barrier, zero=at.partner)

    @pl.when(c == 1)
    def _():
        for d in range(1, widths):
            tell(barrier, width=lax.rem(at.w + d, widths))

    pl.semaphore_wait(barrier, 2 + widths * c)
    pl.when(c == 1)(lambda: tell(ready, zero=at.partner))

    def onward(k):
        p, where = (at.chip_x, at.yn) if k < n else (at.chip_y, at.xn)
        return remote(
            region(units[k], outs, rows, p, c), region(units[k], diag, rows, 0, c), on_send, on_recv.at[k % n], zero=where
        )

    def across(k, early):
        there = region(units[k], diag, rows, 0, c)
        source = region(units[k], outs, rows, at.chip_d, c) if early else there
        return remote(source, there, send, recv, zero=at.partner)

    for j in range(n):
        for k in (j, n + j):
            if j < EARLY:
                pl.when(c == 0)(lambda k=k: onward(k).start())
            else:
                onward(k).start()

    others = every.at[: widths - 1]
    to_partner = remote(every, every, psend, precv, zero=at.partner)

    @pl.when(c == 1)
    def _():
        for d in range(1, widths):
            remote(on, every.at[at.w], nsend, nrecv, width=lax.rem(at.w + d, widths)).start()
        for j in range(EARLY):
            for k in (j, n + j):
                across(k, True).start()
                pltpu.make_async_copy(
                    region(units[k], outs, rows, at.chip_d, c), region(units[k], diag, rows, 0, c), copied
                ).start()
        every[at.w] = on[...]
        arrived(others, nsend)
        arrived(others, nrecv)
        to_partner.start()

    pl.when(c == 0)(lambda: pl.semaphore_wait(ready, 1))
    size = norm.shape[0] // (zeros * widths)
    for j in range(n):
        if j == n - 3:
            pl.when(c == 0)(lambda: to_partner.wait_recv())
            for zero in range(zeros):
                for w in range(widths):
                    i = zero * widths + w
                    flat[:, i * size : (i + 1) * size] = every[w, zero % 2, zero // 2][:, :size]
            norm[...] = flat[0, :].astype(BF16)

        def pass_on():
            a, _, size = units[j]
            arrived(dm.at[:rows, : 2 * size] if a == 3 else dq.at[: 2 * size, :], on_recv.at[j])
            across(j, False).start()
            across(n + j, False).start()

        if j < EARLY:
            pl.when(c == 0)(pass_on)
        else:
            pass_on()

    @pl.when(c == 0)
    def _():
        arrived(share, on_send)

    @pl.when(c == 1)
    def _():
        early = early_rows(units, rows, EARLY)
        if EARLY < n:
            arrived(oq.at[: early_rows(units, rows, n) - early, :], on_send)
        arrived(oq.at[:early, :], copied)
        to_partner.wait_send()

    arrived(share, send)
    arrived(share, recv)


def publish_most(rows, *refs):
    n = 4
    at = Place()
    token, done = refs[-2:]
    token[...] = jnp.zeros_like(token)
    pair = 2 * rows
    for p in (at.chip, at.chip_x, at.chip_y):
        for k, (src, dst) in enumerate(zip(refs[:n], refs[n : 2 * n])):
            block = pl.ds(pl.multiple_of(pair * p, LANES), pair)
            for e in range(2):
                if k == 3:
                    half = src.shape[1] // 2
                    where = (block, slice(e * half, (e + 1) * half))
                else:
                    half = src.shape[0] // 2
                    where = (slice(e * half, (e + 1) * half), block)
                pltpu.make_async_copy(src.at[where], dst.at[where], done.at[k]).start()
    for k, src in enumerate(refs[:n]):
        arrived(src.at[: 3 * pair, :] if k == 3 else src.at[:, : 3 * pair], done.at[k])


def publish_rest(rows, *refs):
    n = 4
    at = Place()
    sources, norm, outs, norm_out, done = refs[:n], refs[n], refs[2 * n + 1 : 3 * n + 1], refs[3 * n + 1], refs[-1]
    pair = 2 * rows
    block = pl.ds(pl.multiple_of(pair * at.chip_d, LANES), pair)
    for e in range(4):
        for k, (src, dst) in enumerate(zip(sources, outs)):
            if k in (1, 2) and e % 2:
                continue
            parts = 2 if k in (1, 2) else 4
            size = src.shape[1 if k == 3 else 0] // parts
            i = e * parts // 4
            if k == 3:
                at_i = slice(i * size, (i + 1) * size)
                pltpu.make_async_copy(src.at[:, at_i], dst.at[block, at_i], done.at[k]).start()
            else:
                at_i = slice(i * size, (i + 1) * size)
                pltpu.make_async_copy(src.at[at_i, :], dst.at[at_i, block], done.at[k]).start()
    pltpu.make_async_copy(norm, norm_out, done.at[n]).start()
    for k, src in enumerate((*sources, norm)):
        arrived(src, done.at[k])


def fast_body(zeros, widths, *args):
    tq, lq, hq, tk, lk, hk, tv, lv, hv, tm, lm, hm, nt, ns = args
    rows, depth = tq.shape[0], tq.shape[0] * zeros
    new = jax.ShapeDtypeStruct
    shapes = [(tq.shape[1], depth), (tk.shape[1], depth), (tv.shape[1], depth), (depth, tm.shape[0])]
    pair = 2 * rows
    held = 2 * sum(a * b for a, b in shapes)
    dma = pltpu.SemaphoreType.DMA
    count = len(unit_list(rows, tm.shape[0], tq.shape[1] // 2, tk.shape[1] // 2))
    moved = [tq, lq.T, hq, tk, lk.T, hk, tv, lv.T, hv, tm.T, lm.T, hm, nt[None, :], ns[None, :]]
    rank, mix = hm.shape[0], tm.shape[0]
    halves = (tq.shape[1] + tk.shape[1] + tv.shape[1]) // 2
    norms = (CORES, zeros // CORES, 1, LANES)
    in_vmem, in_hbm = pl.BlockSpec(memory_space=VMEM), pl.BlockSpec(memory_space=HBM)
    *most, on = pl.pallas_call(
        functools.partial(gather, zeros, widths),
        out_shape=[VMEM(s, BF16) for s in shapes] + [VMEM(norms, F32)],
        in_specs=[in_hbm] * len(args),
        out_specs=[in_vmem] * (len(shapes) + 1),
        scratch_shapes=[
            VMEM((rows, mix), BF16), VMEM((rank, mix + rows), BF16), VMEM((pair, halves), BF16),
            VMEM((3, 2, rank, rows), BF16), VMEM((rank, 2 * halves), BF16), VMEM((2, 1, nt.shape[0]), F32),
            VMEM((tq.shape[1] // 2, pair), BF16), VMEM((tk.shape[1] // 2, pair), BF16), VMEM((tv.shape[1] // 2, pair), BF16),
            VMEM((rows, mix), BF16), VMEM((rank, pair), BF16),
            dma((7,)), dma, dma((2,)), dma((2,)), dma((5,)), dma((count,)), dma((3,)), dma, dma, dma((3,)), dma((3,)),
        ],
        compiler_params=pltpu.CompilerParams(
            collective_id=0, has_side_effects=True, vmem_limit_bytes=VMEM_BYTES - held - 64 * 1024
        ),
        name="gather_merged",
    )(*moved)
    *done, token = pl.pallas_call(
        functools.partial(publish_most, rows),
        out_shape=[new(s, BF16) for s in shapes] + [VMEM((8, LANES), F32)],
        in_specs=[in_vmem] * len(shapes),
        out_specs=[in_hbm] * len(shapes) + [in_vmem],
        scratch_shapes=[dma((len(shapes),))],
        compiler_params=pltpu.CompilerParams(vmem_limit_bytes=2**20),
        name="publish_most",
    )(*most)
    part = [(s[0], pair) for s in shapes[:3]] + [(pair, shapes[3][1])]
    *rest, norm, _ = pl.pallas_call(
        functools.partial(finish, zeros, widths),
        out_shape=[VMEM(s, BF16) for s in part] + [VMEM((depth,), BF16), VMEM((widths, *norms), F32)],
        in_specs=[in_vmem] * (len(shapes) + 2),
        out_specs=[in_vmem] * (len(part) + 2),
        scratch_shapes=[
            VMEM((1, depth), F32), pltpu.SemaphoreType.REGULAR,
            dma, dma, dma((count // 2,)), dma, dma, dma, dma, dma, dma,
        ],
        compiler_params=pltpu.CompilerParams(collective_id=1, has_side_effects=True, vmem_limit_bytes=2**21),
        name="finish",
    )(token, *most, on)
    return pl.pallas_call(
        functools.partial(publish_rest, rows),
        out_shape=[new(s, BF16) for s in shapes] + [new((depth,), BF16)],
        in_specs=[in_vmem] * (len(shapes) + 1) + [in_hbm] * len(shapes),
        out_specs=[in_hbm] * (len(shapes) + 1),
        input_output_aliases={len(shapes) + 1 + k: k for k in range(len(shapes))},
        scratch_shapes=[dma((len(shapes) + 1,))],
        compiler_params=pltpu.CompilerParams(vmem_limit_bytes=2**20),
        name="publish_rest",
    )(*rest, norm, *done)


def solution(mesh):
    placed = (
        P("zero", "width"), P("zero", None), P(None, "width"),
        P("zero", "width"), P("zero", None), P(None, "width"),
        P("zero", "width"), P("zero", None), P(None, "width"),
        P("width", "zero"), P("width", None), P(None, "zero"),
        P(("zero", "width")), P(("zero", "width")),
    )
    zeros, widths = mesh.shape["zero"], mesh.shape["width"]
    side = math.isqrt(zeros // CORES)

    def body(*args):
        rows, nq, nk, mix = args[0].shape[0], args[0].shape[1] // 2, args[3].shape[1] // 2, args[9].shape[0]
        square = side == 2 and CORES * side * side == zeros and args[6].shape == args[3].shape
        even = (2 * nq + 4 * nk) % mix == 0 and rows % 64 == 0
        if square and even and nq % 128 == 0 and nk % 128 == 0 and mix % (4 * LANES) == 0:
            return fast_body(zeros, widths, *args)
        return plain_body(*args)

    return jax.shard_map(
        body,
        mesh=mesh,
        in_specs=placed,
        out_specs=(P("width", None), P("width", None), P("width", None), P(None, "width"), P()),
        check_vma=False,
    )
```

time: 108 us -> 98.4 us (0.911)
  Pallas kernels: 107 us -> 97.6 us
    pallas_call x2 -> x4, Pallas kernels: 107 us -> 97.6 us  [the longest x1 66.6 us: fast_body(): pl.pallas_call(functools.partial(gather, zeros, widths), out_shape=[VMEM(...]
where the time goes in v1:
time: 98.4 us; the launch traced here: 98.3 us
  Pallas kernels  97.6 us (99%)
    pallas_call x1, Pallas kernels, fast_body(): pl.pallas_call(functools.partial(gather, zeros, widths), out_shape=[VMEM(...  66.6 us
    pallas_call x1, Pallas kernels, fast_body(): pl.pallas_call(functools.partial(finish, zeros, widths), out_shape=[VMEM(...  22.8 us
    pallas_call x1, Pallas kernels, fast_body(): pl.pallas_call(functools.partial(publish_most, rows), out_shape=[new(s, B...  5.79 us
    pallas_call x1, Pallas kernels, fast_body(): pl.pallas_call(functools.partial(publish_rest, rows), out_shape=[new(s, B...  2.48 us

profile of v1, /device:TPU:0, one launch (start us, length us, event | category | flops | bytes accessed | tf_op | source)
XLA Modules:
  0.0 98.3 jit_solution(11412044871842455999)
XLA Ops:
  0.6 66.6 %gather_merged.1 = (bf16[1024,3584]{1,0:T(8,128)(2,1)S(1)}, bf16[512,3584]{1,0:T(8,128)(2,1)S(1)}, bf16[512,3584]{1,0:T(8,128)(2,1)S(1)}, bf16[3584,1024]{1,0:T(8,128)(2,1)S(1)}, f32[2,4,1,128]{3,2,1,0:T(1,128)S(1)}) custom-call(bf16[448,1024]{1,0:T(8,128)(2,1)} %tq_h.1, bf16[32,448]{1,0:T(8,128)(2,1)} %bitcast.9, bf16[32,1024]{1,0:T(8,128)(2,1)} %hq_h.1, ...), custom_call_target="tpu_custom_call" | custom-call | tf_op jit(solution)/shard_map/gather_merged/pallas_call | solution.py:432
  67.2 5.8 %publish_most.1 = (bf16[1024,3584]{1,0:T(8,128)(2,1)}, bf16[512,3584]{1,0:T(8,128)(2,1)}, bf16[512,3584]{1,0:T(8,128)(2,1)}, bf16[3584,1024]{1,0:T(8,128)(2,1)}, f32[8,128]{1,0:T(8,128)S(1)}) custom-call(bf16[1024,3584]{1,0:T(8,128)(2,1)S(1)} %get-tuple-element.20.refs_0_.refs_1_, bf16[512,3584]{1,0:T(8,128)(2,1)S(1)} %get-tuple-element.21.refs_1_.refs_2_, ...), custom_call_target="tpu_custom_call" | custom-call | tf_op jit(solution)/shard_map/publish_most/pallas_call | solution.py:449
  73.0 22.8 %finish.1 = (bf16[1024,896]{1,0:T(8,128)(2,1)S(1)}, bf16[512,896]{1,0:T(8,128)(2,1)S(1)}, bf16[512,896]{1,0:T(8,128)(2,1)S(1)}, bf16[896,1024]{1,0:T(8,128)(2,1)...) custom-call(f32[8,128]{1,0:T(8,128)S(1)} %get-tuple-element.24.refs_0_, ...), custom_call_target="tpu_custom_call" | custom-call | tf_op jit(solution)/shard_map/finish/pallas_call | solution.py:459
  95.8 2.5 %publish_rest.1 = (bf16[1024,3584]{1,0:T(8,128)(2,1)}, bf16[512,3584]{1,0:T(8,128)(2,1)}, bf16[512,3584]{1,0:T(8,128)(2,1)}, bf16[3584,1024]{1,0:T(8,128)(2,1)}, bf16[3584]{0:T(1024)(128)(2,1)}) custom-call(bf16[1024,896]{1,0:T(8,128)(2,1)S(1)} %get-tuple-element.26.refs_0_, ...), custom_call_target="tpu_custom_call", output_to_operand_aliasing={{0}: (5, {}), {1}: (6, {}), {2}: (7, {}), {3}: (8, {})} | custom-call | tf_op jit(solution)/shard_map/publish_rest/pallas_call | solution.py:471

commit v2 on v1

v2 whole, which is shorter than its diff:
```python
import functools
import math

import jax
import jax.numpy as jnp
from jax import lax
from jax.experimental import pallas as pl
from jax.experimental.pallas import tpu as pltpu
from jax.sharding import PartitionSpec as P

mix_rate = 0.5
CORES = 2
LANES = 128
F32 = jnp.float32
BF16 = jnp.bfloat16
BOTH = 1
EARLY = 7
VMEM_BYTES = 67_043_328
VMEM = pltpu.VMEM
HBM = pltpu.MemorySpace.HBM
TO_X, TO_Y, ON, P_OWN, P_X, P_Y, P_D = range(7)


def plain_body(
    train_query, low_query, high_query, train_key, low_key, high_key, train_value, low_value, high_value,
    train_mixed, low_mixed, high_mixed, norm_train, norm_step,
):
    def merged(train, low, high):
        return (train.astype(F32) + mix_rate * jnp.dot(low, high, preferred_element_type=F32)).astype(BF16)

    return (
        lax.all_gather(merged(train_query, low_query, high_query), "zero", axis=0, tiled=True).T,
        lax.all_gather(merged(train_key, low_key, high_key), "zero", axis=0, tiled=True).T,
        lax.all_gather(merged(train_value, low_value, high_value), "zero", axis=0, tiled=True).T,
        lax.all_gather(merged(train_mixed, low_mixed, high_mixed).T, "zero", axis=0, tiled=True),
        lax.all_gather((norm_train + norm_step).astype(BF16), ("zero", "width"), axis=0, tiled=True),
    )


class Place:
    def __init__(self):
        self.me, self.w = lax.axis_index("zero"), lax.axis_index("width")
        me = self.me
        self.c = lax.rem(me, 2)
        x = lax.rem(lax.div(me, 2), 2)
        self.y = lax.div(me, 4)
        self.chip = lax.div(me, 2)
        self.partner, self.xn, self.yn = me + 1 - 2 * self.c, me + 2 - 4 * x, me + 4 - 8 * self.y
        self.chip_x, self.chip_y, self.chip_d = self.chip + 1 - 2 * x, self.chip + 2 - 4 * self.y, 3 - self.chip


def remote(src, dst, ssem, rsem, **where):
    return pltpu.make_async_remote_copy(
        src_ref=src, dst_ref=dst, send_sem=ssem, recv_sem=rsem, device_id=where, device_id_type=pl.DeviceIdType.MESH
    )


def tell(sem, **where):
    pl.semaphore_signal(sem, inc=1, device_id=where, device_id_type=pl.DeviceIdType.MESH)


def unit_list(rows, mix, nq, nk):
    eighth = mix // 8
    mixed = ((0, eighth), (eighth, eighth), (2 * eighth, 2 * eighth))
    query = ((0, nq // 4), (nq // 4, nq // 4))
    parts = ((0, nk // 2), (nk // 2, nk // 4), (3 * nk // 4, nk // 8), (7 * nk // 8, nk // 8))
    return [
        (a, at + half, size)
        for key, share in ((1, 0), (2, 1))
        for a, half, pieces in ((3, share * mix // 2, mixed), (0, share * nq // 2, query), (key, 0, parts))
        for at, size in pieces
    ]


def region(unit, outs, rows, chip, c):
    a, start, size = unit
    out = outs[a]
    if a == 3:
        return out.at[pl.ds(pl.multiple_of(rows * (2 * chip + c), 16), rows), start : start + size]
    pair = 2 * rows
    return out.at[
        pl.ds(pl.multiple_of(c * (out.shape[0] // 2) + start, 16), size), pl.ds(pl.multiple_of(pair * chip, LANES), pair)
    ]


def arrived(ref, sem):
    pltpu.make_async_copy(ref, ref, sem).wait()


def gather(
    zeros, widths,
    tq_h, lq_h, hq_h, tk_h, lk_h, hk_h, tv_h, lv_h, hv_h, tm_h, lm_h, hm_h, nt_h, ns_h,
    oq, ok, ov, om, on,
    tm, pair_m, held, lows, highs, gains, own_q, own_k, own_v, own_m, joined,
    fetched, keep, swap_send, swap_recv, send, arrive, across, on_send, on_recv, early_recv, nsend, nrecv,
):
    at = Place()
    c, chip = at.c, at.chip
    rows = tq_h.shape[0]
    pair = 2 * rows
    mix = tm_h.shape[1]
    outs = (oq, ok, ov, om)
    nq, nk = oq.shape[0] // 2, ok.shape[0] // 2
    units = unit_list(rows, mix, nq, nk)
    n = len(units) // 2
    first = units[0][2]
    share = om.at[: rows * (mix + 2 * nq + 4 * nk) // mix, :]
    LOW_HIGH, FIRST, OTHERS, GAINS, LOWS, HIGHS, TRAINS = range(7)

    def rank_dot(left, right):
        return lax.dot_general(left, right, (((0,), (0,)), ((), ())), preferred_element_type=F32)

    def fetch(src, dst, sem):
        pltpu.make_async_copy(src, dst, fetched.at[sem]).start()

    fetch(lm_h, pair_m.at[:, :mix], LOW_HIGH)
    fetch(hm_h, pair_m.at[:, mix:], LOW_HIGH)
    fetch(tm_h.at[:, :first], tm.at[:, :first], FIRST)
    barrier = pltpu.get_barrier_semaphore()
    for other in (at.partner, at.xn, at.yn):
        tell(barrier, zero=other)
    fetch(nt_h, gains.at[0], GAINS)
    fetch(ns_h, gains.at[1], GAINS)
    fetch(tm_h.at[:, first:], tm.at[:, first:], OTHERS)

    mine = pl.ds(pl.multiple_of(rows * c, 16), rows)
    spans, spot = [], 0
    for train in (tq_h, tk_h, tv_h):
        spans.append(slice(spot, spot + train.shape[1] // 2))
        spot += train.shape[1] // 2
    for k, (train, low, high) in enumerate(((tq_h, lq_h, hq_h), (tk_h, lk_h, hk_h), (tv_h, lv_h, hv_h))):
        half = train.shape[1] // 2
        cols = pl.ds(pl.multiple_of(c * half, LANES), half)
        fetch(train.at[:, cols], held.at[mine, spans[k]], TRAINS)
        fetch(low, lows.at[k, c], LOWS)
        fetch(high, highs.at[:, 2 * spans[k].start : 2 * spans[k].stop], HIGHS)

    def merge_mixed(start, size):
        cols = slice(start, start + size)
        merged = tm[:, cols].astype(F32) + mix_rate * rank_dot(pair_m[:, mix:], pair_m[:, cols])
        own_m[:, cols] = merged.astype(BF16)

    sources = [
        own_m.at[:, s : s + size] if a == 3 else (own_q, own_k, own_v)[a].at[s : s + size, :] for a, s, size in units
    ]

    def move(k, kind):
        p = {ON: at.chip_x if k < n else at.chip_y, P_X: at.chip_x, P_Y: at.chip_y, P_D: at.chip_d}.get(kind, chip)
        there = region(units[k], outs, rows, p, c)
        where = {TO_X: at.xn, TO_Y: at.yn, ON: at.yn if k < n else at.xn}.get(kind, at.partner)
        if kind in (TO_X, TO_Y):
            recv = arrive.at[k % n + (n if (kind == TO_X) == (k >= n) else 0)]
        elif kind == ON:
            recv = on_recv.at[k % n] if k % n < BOTH else early_recv
        else:
            recv = across.at[kind - P_OWN]
        return remote(
            sources[k] if kind in (TO_X, TO_Y, P_OWN) else there, there,
            on_send if kind == ON else send.at[kind - (kind > ON)], recv, zero=where,
        )

    def come(j, sem):
        a, _, size = units[j]
        arrived(om.at[:rows, : 2 * size] if a == 3 else oq.at[: 2 * size, :pair], sem)

    arrived(pair_m, fetched.at[LOW_HIGH])
    arrived(tm.at[:, :first], fetched.at[FIRST])
    merge_mixed(0, first)

    pl.semaphore_wait(barrier, 3)
    move(0, TO_X).start()
    move(0, TO_Y).start()
    for k, (train, low) in enumerate(((tq_h, lq_h), (tk_h, lk_h), (tv_h, lv_h))):
        half = train.shape[1] // 2
        cols = pl.ds(pl.multiple_of((1 - c) * half, LANES), half)
        remote(train.at[:, cols], held.at[mine, spans[k]], swap_send.at[0], swap_recv.at[0], zero=at.partner).start()
        remote(low, lows.at[k, c], swap_send.at[1], swap_recv.at[1], zero=at.partner).start()

    arrived(gains, fetched.at[GAINS])
    on[c, chip] = jnp.pad(gains[0] + gains[1], ((0, 0), (0, LANES - gains.shape[2])))
    arrived(tm.at[:, first:], fetched.at[OTHERS])
    for k in (n, 1, n + 1, 2, n + 2):
        merge_mixed(*units[k][1:])

    row = on.at[c, pl.ds(chip, 1)]
    both_rows = on.at[c, pl.ds(2 * at.y, 2)]
    small = [
        remote(row, row, nsend.at[0], nrecv.at[0], zero=at.xn),
        remote(both_rows, both_rows, nsend.at[1], nrecv.at[1], zero=at.yn),
        remote(on.at[c], on.at[c], nsend.at[2], nrecv.at[2], zero=at.partner),
    ]
    small[0].start()
    move(n, TO_Y).start()
    for j in (1, 2):
        move(j, TO_X).start()
        move(n + j, TO_Y).start()

    def keep_own(source, there):
        pltpu.make_async_copy(source, there, keep).start()

    keep_own(own_m, om.at[pl.ds(pl.multiple_of(rows * at.me, 16), rows), :])

    def merge(e, out, own_out):
        span = spans[e]
        half = span.stop - span.start
        joined[:, :rows] = lows[e, 0]
        joined[:, rows:] = lows[e, 1]
        cols = pl.ds(pl.multiple_of(2 * span.start + c * half, LANES), half)
        for j in range(pair // LANES):
            part = slice(j * LANES, (j + 1) * LANES)
            merged = held[part, span].astype(F32) + mix_rate * rank_dot(joined[:, part], highs[:, cols])
            own_out[:, part] = merged.T.astype(BF16)
        keep_own(own_out, out.at[
            pl.ds(pl.multiple_of(c * half, 16), half), pl.ds(pl.multiple_of(pair * chip, LANES), pair)
        ])

    theirs = pl.ds(pl.multiple_of(rows * (1 - c), 16), rows)
    arrived(lows.at[:, 0], fetched.at[LOWS])
    arrived(highs, fetched.at[HIGHS])
    arrived(held.at[mine, :], fetched.at[TRAINS])
    arrived(lows.at[:, 0], swap_recv.at[1])
    arrived(held.at[theirs, :], swap_recv.at[0])
    merge(0, oq, own_q)
    for j in (3, 4):
        move(j, TO_X).start()
        move(n + j, TO_Y).start()
    merge(1, ok, own_k)
    merge(2, ov, own_v)
    for j in range(5, n):
        move(j, TO_X).start()
        move(n + j, TO_Y).start()
    small[0].wait()
    small[1].start()
    for j in range(n):
        move(n + j, TO_X).start()
        if j > 0:
            move(j, TO_Y).start()
    for k in range(2 * n):
        move(k, P_OWN).start()

    def onward(j):
        move(j, ON).start()
        move(n + j, ON).start()

    for j in range(n):
        come(j, arrive.at[j])
        if j < BOTH:
            onward(j)
        elif j < EARLY:
            pl.when(c == 1)(lambda j=j: onward(j))
        move(j, P_X).start()
        move(n + j, P_Y).start()
    small[1].wait()
    small[2].start()
    arrived(lows.at[:, 0], swap_send.at[1])
    arrived(held.at[mine, :], swap_send.at[0])
    arrived(share, keep)
    small[2].wait()
    for j in range(n):
        come(j, arrive.at[n + j])
        move(n + j, P_X).start()
        move(j, P_Y).start()
    for j in range(BOTH):
        come(j, on_recv.at[j])
        move(j, P_D).start()
        move(n + j, P_D).start()
    for kind in range(5):
        arrived(share, send.at[kind])
    for kind in range(3):
        arrived(share, across.at[kind])
    common, early = early_rows(units, rows, BOTH), early_rows(units, rows, EARLY)
    if BOTH:
        arrived(oq.at[:common, :], send.at[5])
        arrived(oq.at[:common, :], across.at[3])
        pl.when(c == 0)(lambda: arrived(oq.at[:common, :], on_send))

    @pl.when(c == 1)
    def _():
        arrived(oq.at[:early, :], on_send)
        arrived(oq.at[: early - common, :], early_recv)


def early_rows(units, rows, count):
    return 2 * sum(size * rows if a == 3 else size * 2 * rows for a, _, size in units[:count]) // (8 * rows)


def finish(zeros, widths, *refs):
    (
        _, oq, ok, ov, om, on, dq, dk, dv, dm, norm,
        every, flat, ready, copied, on_send, on_recv, send, recv, nsend, nrecv,
    ) = refs
    at = Place()
    c = at.c
    outs, diag = (oq, ok, ov, om), (dq, dk, dv, dm)
    rows = dm.shape[0] // 2
    units = unit_list(rows, om.shape[1], oq.shape[0] // 2, ok.shape[0] // 2)
    n = len(units) // 2
    common, early, whole = (early_rows(units, rows, count) for count in (BOTH, EARLY, n))

    barrier = pltpu.get_barrier_semaphore()
    for other in (at.xn, at.yn):
        tell(barrier, zero=other)
    pl.when(c == 0)(lambda: tell(barrier, zero=at.partner))

    @pl.when(c == 1)
    def _():
        for d in range(1, widths):
            tell(barrier, width=lax.rem(at.w + d, widths))

    pl.semaphore_wait(barrier, 2 + widths * c)
    pl.when(c == 1)(lambda: tell(ready, zero=at.partner))

    def onward(j):
        for k in (j, n + j):
            p, where = (at.chip_x, at.yn) if k < n else (at.chip_y, at.xn)
            source, there = region(units[k], outs, rows, p, c), region(units[k], diag, rows, 0, c)
            remote(source, there, on_send, on_recv.at[j], zero=where).start()

    def across(j, early):
        for k in (j, n + j):
            there = region(units[k], diag, rows, 0, c)
            source = region(units[k], outs, rows, at.chip_d, c) if early else there
            remote(source, there, send, recv, zero=at.partner).start()
            if early:
                pltpu.make_async_copy(source, there, copied).start()

    for j in range(BOTH, n):
        if j < EARLY:
            pl.when(c == 0)(lambda j=j: onward(j))
        else:
            onward(j)

    to_partner = remote(every, every, nsend.at[0], nrecv.at[0], zero=at.partner)

    @pl.when(c == 1)
    def _():
        for d in range(1, widths):
            remote(on, every.at[at.w], nsend.at[1], nrecv.at[1], width=lax.rem(at.w + d, widths)).start()
        for j in range(BOTH, EARLY):
            across(j, True)
        every[at.w] = on[...]
        for sems in (nsend, nrecv):
            arrived(every.at[: widths - 1], sems.at[1])
        to_partner.start()

    pl.when(c == 0)(lambda: pl.semaphore_wait(ready, 1))
    size = norm.shape[0] // (zeros * widths)
    for j in range(BOTH, n):
        if j == n - 3:
            pl.when(c == 0)(lambda: to_partner.wait_recv())
            for zero in range(zeros):
                for w in range(widths):
                    i = zero * widths + w
                    flat[:, i * size : (i + 1) * size] = every[w, zero % 2, zero // 2][:, :size]
            norm[...] = flat[0, :].astype(BF16)

        def pass_on():
            a, _, size = units[j]
            arrived(dm.at[:rows, : 2 * size] if a == 3 else dq.at[: 2 * size, :], on_recv.at[j])
            across(j, False)

        if j < EARLY:
            pl.when(c == 0)(pass_on)
        else:
            pass_on()

    pl.when(c == 0)(lambda: arrived(oq.at[: whole - common, :], on_send))

    @pl.when(c == 1)
    def _():
        if EARLY < n:
            arrived(oq.at[: whole - early, :], on_send)
        arrived(oq.at[: early - common, :], copied)
        to_partner.wait_send()

    arrived(oq.at[: whole - common, :], send)
    arrived(oq.at[: whole - common, :], recv)


def publish_most(rows, *refs):
    n = 4
    at = Place()
    sources, outs, token, done = refs[:n], refs[n : 2 * n], *refs[2 * n :]
    token[...] = jnp.zeros_like(token)
    pair = 2 * rows
    for p in (at.chip, at.chip_x, at.chip_y):
        for k, (src, dst) in enumerate(zip(sources, outs)):
            block = pl.ds(pl.multiple_of(pair * p, LANES), pair)
            for e in range(2):
                if k == 3:
                    half = src.shape[1] // 2
                    where = (block, slice(e * half, (e + 1) * half))
                else:
                    half = src.shape[0] // 2
                    where = (slice(e * half, (e + 1) * half), block)
                pltpu.make_async_copy(src.at[where], dst.at[where], done.at[k]).start()
    oq, ok, _, om = sources
    units = unit_list(rows, om.shape[1], oq.shape[0] // 2, ok.shape[0] // 2)
    for k, unit in enumerate(units):
        if k % (len(units) // 2) < BOTH:
            for core in range(CORES):
                src, dst = (region(unit, arrays, rows, at.chip_d, core) for arrays in (sources, outs))
                pltpu.make_async_copy(src, dst, done.at[n]).start()
    for k, src in enumerate(sources):
        arrived(src.at[: 3 * pair, :] if k == 3 else src.at[:, : 3 * pair], done.at[k])
    if BOTH:
        arrived(oq.at[: 2 * early_rows(units, rows, BOTH), :], done.at[n])


def publish_rest(rows, *refs):
    n = 4
    at = Place()
    sources, norm, outs, norm_out, done = refs[:n], refs[n], refs[2 * n + 1 : 3 * n + 1], *refs[3 * n + 1 :]
    oq, ok, _, om = outs
    units = unit_list(rows, om.shape[1], oq.shape[0] // 2, ok.shape[0] // 2)
    half = len(units) // 2
    for j in range(BOTH, half):
        for k in (j, half + j):
            for core in range(CORES):
                src, dst = region(units[k], sources, rows, 0, core), region(units[k], outs, rows, at.chip_d, core)
                pltpu.make_async_copy(src, dst, done.at[0]).start()
    pltpu.make_async_copy(norm, norm_out, done.at[1]).start()
    arrived(oq.at[: 2 * (early_rows(units, rows, half) - early_rows(units, rows, BOTH)), :], done.at[0])
    arrived(norm, done.at[1])


def fast_body(zeros, widths, *args):
    tq, lq, hq, tk, lk, hk, tv, lv, hv, tm, lm, hm, nt, ns = args
    rows, depth = tq.shape[0], tq.shape[0] * zeros
    new = jax.ShapeDtypeStruct
    shapes = [(tq.shape[1], depth), (tk.shape[1], depth), (tv.shape[1], depth), (depth, tm.shape[0])]
    pair = 2 * rows
    held = 2 * sum(a * b for a, b in shapes)
    dma = pltpu.SemaphoreType.DMA
    count = len(unit_list(rows, tm.shape[0], tq.shape[1] // 2, tk.shape[1] // 2))
    moved = [tq, lq.T, hq, tk, lk.T, hk, tv, lv.T, hv, tm.T, lm.T, hm, nt[None, :], ns[None, :]]
    rank, mix = hm.shape[0], tm.shape[0]
    halves = (tq.shape[1] + tk.shape[1] + tv.shape[1]) // 2
    norms = (CORES, zeros // CORES, 1, LANES)
    in_vmem, in_hbm = pl.BlockSpec(memory_space=VMEM), pl.BlockSpec(memory_space=HBM)
    *most, on = pl.pallas_call(
        functools.partial(gather, zeros, widths),
        out_shape=[VMEM(s, BF16) for s in shapes] + [VMEM(norms, F32)],
        in_specs=[in_hbm] * len(args),
        out_specs=[in_vmem] * (len(shapes) + 1),
        scratch_shapes=[
            VMEM((rows, mix), BF16), VMEM((rank, mix + rows), BF16), VMEM((pair, halves), BF16),
            VMEM((3, 2, rank, rows), BF16), VMEM((rank, 2 * halves), BF16), VMEM((2, 1, nt.shape[0]), F32),
            VMEM((tq.shape[1] // 2, pair), BF16), VMEM((tk.shape[1] // 2, pair), BF16), VMEM((tv.shape[1] // 2, pair), BF16),
            VMEM((rows, mix), BF16), VMEM((rank, pair), BF16),
            dma((7,)), dma, dma((2,)), dma((2,)), dma((6,)), dma((count,)), dma((4,)),
            dma, dma((max(BOTH, 1),)), dma, dma((3,)), dma((3,)),
        ],
        compiler_params=pltpu.CompilerParams(
            collective_id=0, has_side_effects=True, vmem_limit_bytes=VMEM_BYTES - held - 64 * 1024
        ),
        name="gather_merged",
    )(*moved)
    *done, token = pl.pallas_call(
        functools.partial(publish_most, rows),
        out_shape=[new(s, BF16) for s in shapes] + [VMEM((8, LANES), F32)],
        in_specs=[in_vmem] * len(shapes),
        out_specs=[in_hbm] * len(shapes) + [in_vmem],
        scratch_shapes=[dma((len(shapes) + 1,))],
        compiler_params=pltpu.CompilerParams(vmem_limit_bytes=2**20),
        name="publish_most",
    )(*most)
    part = [(s[0], pair) for s in shapes[:3]] + [(pair, shapes[3][1])]
    *rest, norm = pl.pallas_call(
        functools.partial(finish, zeros, widths),
        out_shape=[VMEM(s, BF16) for s in part] + [VMEM((depth,), BF16)],
        in_specs=[in_vmem] * (len(shapes) + 2),
        out_specs=[in_vmem] * (len(part) + 1),
        scratch_shapes=[
            VMEM((widths, *norms), F32), VMEM((1, depth), F32),
            pltpu.SemaphoreType.REGULAR, dma, dma, dma((count // 2,)), dma, dma, dma((2,)), dma((2,)),
        ],
        compiler_params=pltpu.CompilerParams(collective_id=1, has_side_effects=True, vmem_limit_bytes=2**20),
        name="finish",
    )(token, *most, on)
    return pl.pallas_call(
        functools.partial(publish_rest, rows),
        out_shape=[new(s, BF16) for s in shapes] + [new((depth,), BF16)],
        in_specs=[in_vmem] * (len(shapes) + 1) + [in_hbm] * len(shapes),
        out_specs=[in_hbm] * (len(shapes) + 1),
        input_output_aliases={len(shapes) + 1 + k: k for k in range(len(shapes))},
        scratch_shapes=[dma((2,))],
        compiler_params=pltpu.CompilerParams(vmem_limit_bytes=2**20),
        name="publish_rest",
    )(*rest, norm, *done)


def solution(mesh):
    placed = (
        P("zero", "width"), P("zero", None), P(None, "width"),
        P("zero", "width"), P("zero", None), P(None, "width"),
        P("zero", "width"), P("zero", None), P(None, "width"),
        P("width", "zero"), P("width", None), P(None, "zero"),
        P(("zero", "width")), P(("zero", "width")),
    )
    zeros, widths = mesh.shape["zero"], mesh.shape["width"]
    side = math.isqrt(zeros // CORES)

    def body(*args):
        rows, nq, nk, mix = args[0].shape[0], args[0].shape[1] // 2, args[3].shape[1] // 2, args[9].shape[0]
        square = side == 2 and CORES * side * side == zeros and args[6].shape == args[3].shape
        even = (2 * nq + 4 * nk) % mix == 0 and rows % 64 == 0
        if square and even and nq % 128 == 0 and nk % 128 == 0 and mix % (8 * LANES) == 0:
            return fast_body(zeros, widths, *args)
        return plain_body(*args)

    return jax.shard_map(
        body,
        mesh=mesh,
        in_specs=placed,
        out_specs=(P("width", None), P("width", None), P("width", None), P(None, "width"), P()),
        check_vma=False,
    )
```

time: 98.4 us -> 97.5 us (level)
    pallas_call x1, Pallas kernels: 22.8 us -> 19.4 us  [fast_body(): pl.pallas_call(functools.partial(finish, zeros, widths), out_shape=[VMEM(...]
    pallas_call x1, Pallas kernels: 66.6 us -> 69.1 us  [fast_body(): pl.pallas_call(functools.partial(gather, zeros, widths), out_shape=[VMEM(...]
where the time goes in v2:
time: 97.5 us; the launch traced here: 97.3 us
  Pallas kernels  96.7 us (99%)
    pallas_call x1, Pallas kernels, fast_body(): pl.pallas_call(functools.partial(gather, zeros, widths), out_shape=[VMEM(...  69.1 us
    pallas_call x1, Pallas kernels, fast_body(): pl.pallas_call(functools.partial(finish, zeros, widths), out_shape=[VMEM(...  19.4 us
    pallas_call x1, Pallas kernels, fast_body(): pl.pallas_call(functools.partial(publish_most, rows), out_shape=[new(s, B...  5.91 us
    pallas_call x1, Pallas kernels, fast_body(): pl.pallas_call(functools.partial(publish_rest, rows), out_shape=[new(s, B...  2.27 us

profile of v2, /device:TPU:0, one launch (start us, length us, event | category | flops | bytes accessed | tf_op | source)
XLA Modules:
  0.0 97.3 jit_solution(7856451674991986774)
XLA Ops:
  0.6 69.1 %gather_merged.1 = (bf16[1024,3584]{1,0:T(8,128)(2,1)S(1)}, bf16[512,3584]{1,0:T(8,128)(2,1)S(1)}, bf16[512,3584]{1,0:T(8,128)(2,1)S(1)}, bf16[3584,1024]{1,0:T(8,128)(2,1)S(1)}, f32[2,4,1,128]{3,2,1,0:T(1,128)S(1)}) custom-call(bf16[448,1024]{1,0:T(8,128)(2,1)} %tq_h.1, bf16[32,448]{1,0:T(8,128)(2,1)} %bitcast.9, bf16[32,1024]{1,0:T(8,128)(2,1)} %hq_h.1, ...), custom_call_target="tpu_custom_call" | custom-call | tf_op jit(solution)/shard_map/gather_merged/pallas_call | solution.py:441
  69.7 5.9 %publish_most.1 = (bf16[1024,3584]{1,0:T(8,128)(2,1)}, bf16[512,3584]{1,0:T(8,128)(2,1)}, bf16[512,3584]{1,0:T(8,128)(2,1)}, bf16[3584,1024]{1,0:T(8,128)(2,1)}, f32[8,128]{1,0:T(8,128)S(1)}) custom-call(bf16[1024,3584]{1,0:T(8,128)(2,1)S(1)} %get-tuple-element.20.refs_0_.refs_1_, bf16[512,3584]{1,0:T(8,128)(2,1)S(1)} %get-tuple-element.21.refs_1_.refs_2_, ...), custom_call_target="tpu_custom_call" | custom-call | tf_op jit(solution)/shard_map/publish_most/pallas_call | solution.py:459
  75.7 19.4 %finish.1 = (bf16[1024,896]{1,0:T(8,128)(2,1)S(1)}, bf16[512,896]{1,0:T(8,128)(2,1)S(1)}, bf16[512,896]{1,0:T(8,128)(2,1)S(1)}, bf16[896,1024]{1,0:T(8,128)(2,1)S(1)}, bf16[3584]{0:T(1024)(128)(2,1)S(1)}) custom-call(f32[8,128]{1,0:T(8,128)S(1)} %get-tuple-element.24.refs_0_, bf16[1024,3584]{1,0:T(8,128)(2,1)S(1)} %get-tuple-element.20.refs_0_.refs_1_, ...), custom_call_target="tpu_custom_call" | custom-call | tf_op jit(solution)/shard_map/finish/pallas_call | solution.py:469
  95.0 2.3 %publish_rest.1 = (bf16[1024,3584]{1,0:T(8,128)(2,1)}, bf16[512,3584]{1,0:T(8,128)(2,1)}, bf16[512,3584]{1,0:T(8,128)(2,1)}, bf16[3584,1024]{1,0:T(8,128)(2,1)}, bf16[3584]{0:T(1024)(128)(2,1)}) custom-call(bf16[1024,896]{1,0:T(8,128)(2,1)S(1)} %get-tuple-element.26.refs_0_, ...), custom_call_target="tpu_custom_call", output_to_operand_aliasing={{0}: (5, {}), {1}: (6, {}), {2}: (7, {}), {3}: (8, {})} | custom-call | tf_op jit(solution)/shard_map/publish_rest/pallas_call | solution.py:481

commit v3 on v2

v3 whole, which is shorter than its diff:
```python
import functools
import math

import jax
import jax.numpy as jnp
from jax import lax
from jax.experimental import pallas as pl
from jax.experimental.pallas import tpu as pltpu
from jax.sharding import PartitionSpec as P

mix_rate = 0.5
CORES = 2
LANES = 128
F32 = jnp.float32
BF16 = jnp.bfloat16
AHEAD = 8
BOTH = 3
EARLY = 9
TWICE = 1
VMEM_BYTES = 67_043_328
VMEM = pltpu.VMEM
HBM = pltpu.MemorySpace.HBM


def plain_body(
    train_query, low_query, high_query, train_key, low_key, high_key, train_value, low_value, high_value,
    train_mixed, low_mixed, high_mixed, norm_train, norm_step,
):
    def merged(train, low, high):
        return (train.astype(F32) + mix_rate * jnp.dot(low, high, preferred_element_type=F32)).astype(BF16)

    return (
        lax.all_gather(merged(train_query, low_query, high_query), "zero", axis=0, tiled=True).T,
        lax.all_gather(merged(train_key, low_key, high_key), "zero", axis=0, tiled=True).T,
        lax.all_gather(merged(train_value, low_value, high_value), "zero", axis=0, tiled=True).T,
        lax.all_gather(merged(train_mixed, low_mixed, high_mixed).T, "zero", axis=0, tiled=True),
        lax.all_gather((norm_train + norm_step).astype(BF16), ("zero", "width"), axis=0, tiled=True),
    )


class Place:
    def __init__(self):
        self.me, self.w = lax.axis_index("zero"), lax.axis_index("width")
        me = self.me
        self.c = lax.rem(me, 2)
        x = lax.rem(lax.div(me, 2), 2)
        self.y = lax.div(me, 4)
        self.chip = lax.div(me, 2)
        self.partner, self.xn, self.yn = me + 1 - 2 * self.c, me + 2 - 4 * x, me + 4 - 8 * self.y
        self.chip_x, self.chip_y, self.chip_d = self.chip + 1 - 2 * x, self.chip + 2 - 4 * self.y, 3 - self.chip


def remote(src, dst, ssem, rsem, **where):
    return pltpu.make_async_remote_copy(
        src_ref=src, dst_ref=dst, send_sem=ssem, recv_sem=rsem, device_id=where, device_id_type=pl.DeviceIdType.MESH
    )


def tell(sem, **where):
    pl.semaphore_signal(sem, inc=1, device_id=where, device_id_type=pl.DeviceIdType.MESH)


def unit_list(rows, mix, nq, nk):
    eighth = mix // 8
    mixed = ((0, eighth), (eighth, 2 * eighth), (3 * eighth, eighth))
    query = ((0, nq // 4), (nq // 4, nq // 4))
    parts = ((0, nk // 2), (nk // 2, nk // 4), (3 * nk // 4, nk // 8), (7 * nk // 8, nk // 8))
    return [
        (a, at + half, size)
        for key, share in ((1, 0), (2, 1))
        for a, half, pieces in ((3, share * mix // 2, mixed), (0, share * nq // 2, query), (key, 0, parts))
        for at, size in pieces
    ]


def region(unit, outs, rows, chip, c):
    a, start, size = unit
    out = outs[a]
    if a == 3:
        return out.at[pl.ds(pl.multiple_of(rows * (2 * chip + c), 16), rows), start : start + size]
    pair = 2 * rows
    return out.at[
        pl.ds(pl.multiple_of(c * (out.shape[0] // 2) + start, 16), size), pl.ds(pl.multiple_of(pair * chip, LANES), pair)
    ]


def arrived(ref, sem):
    pltpu.make_async_copy(ref, ref, sem).wait()


def gather(
    zeros, widths,
    tq_h, lq_h, hq_h, tk_h, lk_h, hk_h, tv_h, lv_h, hv_h, tm_h, lm_h, hm_h, nt_h, ns_h,
    oq, ok, ov, om, on,
    tm, pair_m, held, lows, highs, gains, own_q, own_k, own_v, own_m, joined,
    fetched, keep, swap_send, swap_recv, send, arrive, ahead_send, ahead_recv, cross_send, cross_recv, nsend, nrecv,
):
    at = Place()
    c, chip = at.c, at.chip
    rows = tq_h.shape[0]
    pair = 2 * rows
    mix = tm_h.shape[1]
    outs = (oq, ok, ov, om)
    nq, nk = oq.shape[0] // 2, ok.shape[0] // 2
    units = unit_list(rows, mix, nq, nk)
    n = len(units) // 2
    first = units[0][2]
    LOW_HIGH, FIRST, OTHERS, GAINS, LOWS, HIGHS, TRAINS = range(7)

    def rank_dot(left, right):
        return lax.dot_general(left, right, (((0,), (0,)), ((), ())), preferred_element_type=F32)

    def fetch(src, dst, sem):
        pltpu.make_async_copy(src, dst, fetched.at[sem]).start()

    fetch(lm_h, pair_m.at[:, :mix], LOW_HIGH)
    fetch(hm_h, pair_m.at[:, mix:], LOW_HIGH)
    fetch(tm_h.at[:, :first], tm.at[:, :first], FIRST)
    barrier = pltpu.get_barrier_semaphore()
    for other in (at.partner, at.xn, at.yn):
        tell(barrier, zero=other)
    fetch(nt_h, gains.at[0], GAINS)
    fetch(ns_h, gains.at[1], GAINS)
    fetch(tm_h.at[:, first:], tm.at[:, first:], OTHERS)

    mine = pl.ds(pl.multiple_of(rows * c, 16), rows)
    spans, spot = [], 0
    for train in (tq_h, tk_h, tv_h):
        spans.append(slice(spot, spot + train.shape[1] // 2))
        spot += train.shape[1] // 2
    for k, (train, low, high) in enumerate(((tq_h, lq_h, hq_h), (tk_h, lk_h, hk_h), (tv_h, lv_h, hv_h))):
        half = train.shape[1] // 2
        cols = pl.ds(pl.multiple_of(c * half, LANES), half)
        fetch(train.at[:, cols], held.at[mine, spans[k]], TRAINS)
        fetch(low, lows.at[k, c], LOWS)
        fetch(high, highs.at[:, 2 * spans[k].start : 2 * spans[k].stop], HIGHS)

    def merge_mixed(start, size):
        cols = slice(start, start + size)
        merged = tm[:, cols].astype(F32) + mix_rate * rank_dot(pair_m[:, mix:], pair_m[:, cols])
        own_m[:, cols] = merged.astype(BF16)

    sources = [
        own_m.at[:, s : s + size] if a == 3 else (own_q, own_k, own_v)[a].at[s : s + size, :] for a, s, size in units
    ]

    def link(k, along_x, ssem, rsem):
        there = region(units[k], outs, rows, chip, c)
        remote(sources[k], there, ssem, rsem, zero=at.xn if along_x else at.yn).start()

    def to_x(k):
        link(k, True, send, arrive.at[k])

    def to_y(k):
        link(k, False, send, arrive.at[k - n if k >= n else n])

    def cross(k, p):
        there = region(units[k], outs, rows, p, c)
        remote(sources[k] if p is chip else there, there, cross_send, cross_recv, zero=at.partner).start()

    arrived(pair_m, fetched.at[LOW_HIGH])
    arrived(tm.at[:, :first], fetched.at[FIRST])
    merge_mixed(0, first)

    pl.semaphore_wait(barrier, 3)
    to_x(0)
    to_y(0)
    for k, (train, low) in enumerate(((tq_h, lq_h), (tk_h, lk_h), (tv_h, lv_h))):
        half = train.shape[1] // 2
        cols = pl.ds(pl.multiple_of((1 - c) * half, LANES), half)
        remote(train.at[:, cols], held.at[mine, spans[k]], swap_send.at[0], swap_recv.at[0], zero=at.partner).start()
        remote(low, lows.at[k, c], swap_send.at[1], swap_recv.at[1], zero=at.partner).start()

    arrived(gains, fetched.at[GAINS])
    on[c, chip] = jnp.pad(gains[0] + gains[1], ((0, 0), (0, LANES - gains.shape[2])))
    arrived(tm.at[:, first:], fetched.at[OTHERS])
    for k in (n, 1, n + 1, 2, n + 2):
        merge_mixed(*units[k][1:])

    row = on.at[c, pl.ds(chip, 1)]
    both_rows = on.at[c, pl.ds(2 * at.y, 2)]
    small = [
        remote(row, row, nsend.at[0], nrecv.at[0], zero=at.xn),
        remote(both_rows, both_rows, nsend.at[1], nrecv.at[1], zero=at.yn),
        remote(on.at[c], on.at[c], nsend.at[2], nrecv.at[2], zero=at.partner),
    ]
    small[0].start()
    to_y(n)
    for j in (1, 2):
        to_x(j)
        to_y(n + j)

    def keep_own(source, there):
        pltpu.make_async_copy(source, there, keep).start()

    keep_own(own_m, om.at[pl.ds(pl.multiple_of(rows * at.me, 16), rows), :])

    def merge(e, out, own_out):
        span = spans[e]
        half = span.stop - span.start
        joined[:, :rows] = lows[e, 0]
        joined[:, rows:] = lows[e, 1]
        cols = pl.ds(pl.multiple_of(2 * span.start + c * half, LANES), half)
        for j in range(pair // LANES):
            part = slice(j * LANES, (j + 1) * LANES)
            merged = held[part, span].astype(F32) + mix_rate * rank_dot(joined[:, part], highs[:, cols])
            own_out[:, part] = merged.T.astype(BF16)
        keep_own(own_out, out.at[
            pl.ds(pl.multiple_of(c * half, 16), half), pl.ds(pl.multiple_of(pair * chip, LANES), pair)
        ])

    theirs = pl.ds(pl.multiple_of(rows * (1 - c), 16), rows)
    arrived(lows.at[:, 0], fetched.at[LOWS])
    arrived(highs, fetched.at[HIGHS])
    arrived(held.at[mine, :], fetched.at[TRAINS])
    arrived(lows.at[:, 0], swap_recv.at[1])
    arrived(held.at[theirs, :], swap_recv.at[0])
    merge(0, oq, own_q)
    small[0].wait()
    small[1].start()
    for j in (3, 4):
        to_x(j)
        to_y(n + j)
    merge(1, ok, own_k)
    merge(2, ov, own_v)
    for j in range(5, n):
        to_x(j)
        to_y(n + j)
    @pl.when(c == 1)
    def _():
        for j in range(AHEAD):
            for k in second_pair(j, n):
                link(k, k >= n, ahead_send, ahead_recv)

    for k in range(2 * n):
        cross(k, chip)
    lists = rows_of(units[:n])
    for j in range(n):
        arrived(oq.at[: rows_of([units[j]] * 2), :], arrive.at[j])
        cross(j, at.chip_x)
        cross(n + j, at.chip_y)
        if j == 0:
            arrived(oq.at[: rows_of(units[:1]), :], arrive.at[n])
            cross(0, at.chip_y)
        if j == n - 4:
            small[1].wait()
            small[2].start()
    arrived(lows.at[:, 0], swap_send.at[1])
    arrived(held.at[mine, :], swap_send.at[0])
    arrived(oq.at[: 2 * lists, :], keep)
    small[2].wait()
    phase = oq.at[: 2 * lists + rows_of(units[:1]), :]
    arrived(phase, send)
    arrived(oq.at[: 4 * lists + rows_of(units[:1]), :], cross_send)
    arrived(oq.at[: 4 * lists + rows_of(units[:1]), :], cross_recv)

    @pl.when(c == 1)
    def _():
        ahead = oq.at[: rows_of([units[k] for j in range(AHEAD) for k in second_pair(j, n)]), :]
        arrived(ahead, ahead_send)
        arrived(ahead, ahead_recv)


def second_pair(j, n):
    return (n + j, j) if j else (n,)


def rows_of(units):
    return sum(size // 8 if a == 3 else size // 4 for a, _, size in units)


def enter(at, z_peers, ready, told):
    c = at.c
    barrier = pltpu.get_barrier_semaphore()
    for other in (at.xn, at.yn):
        tell(barrier, zero=other)

    @pl.when(c == 1)
    def _():
        for w in z_peers:
            tell(barrier, width=w)

    pl.semaphore_wait(barrier, 2 + (1 + len(z_peers)) * c)
    pl.when(c == 0)(lambda: tell(barrier, zero=at.partner))

    @pl.when(c == 1)
    def _():
        for other in told:
            tell(ready, zero=other)


def spread(zeros, widths, *refs):
    (
        _, oq, ok, ov, om, on, xq, xk, xv, xm, yq, yk, yv, ym, dq, dk, dv, dm, norm,
        every, flat, ready, copied, send, arrive, on_send, on_recv, early_recv, cross_send, cross_recv, nsend, nrecv,
    ) = refs
    at = Place()
    c = at.c
    outs, from_x, from_y, diag = (oq, ok, ov, om), (xq, xk, xv, xm), (yq, yk, yv, ym), (dq, dk, dv, dm)
    rows = dm.shape[0] // 2
    units = unit_list(rows, om.shape[1], oq.shape[0] // 2, ok.shape[0] // 2)
    n = len(units) // 2
    z_peers = [lax.rem(at.w + d, widths) for d in range(1, widths)]
    enter(at, z_peers, ready, [at.partner])

    def own(j):
        for k in second_pair(j, n):
            source = region(units[k], outs, rows, at.chip, c)
            there = region(units[k], from_x if k >= n else from_y, rows, 0, c)
            remote(source, there, send, arrive.at[j], zero=at.xn if k >= n else at.yn).start()

    def onward(j):
        for k in (j, n + j):
            source = region(units[k], outs, rows, at.chip_x if k < n else at.chip_y, c)
            there = region(units[k], diag, rows, 0, c)
            recv = on_recv.at[j] if j < BOTH else early_recv
            remote(source, there, on_send, recv, zero=at.yn if k < n else at.xn).start()

    def across(j, ahead):
        for k in second_pair(j, n):
            there = region(units[k], from_x if k >= n else from_y, rows, 0, c)
            source = region(units[k], outs, rows, at.chip_x if k >= n else at.chip_y, c) if ahead else there
            remote(source, there, cross_send, cross_recv, zero=at.partner).start()
            if ahead:
                pltpu.make_async_copy(source, there, copied).start()

    def some(core_0_alone, step):
        pl.when(c == 0)(step) if core_0_alone else step()

    for j in range(n):
        some(j < AHEAD, lambda: own(j))
    for j in range(BOTH):
        onward(j)
    to_partner = remote(every, every, nsend.at[0], nrecv.at[0], zero=at.partner)

    @pl.when(c == 1)
    def _():
        for j in range(BOTH, EARLY):
            onward(j)
        for w in z_peers:
            remote(on, every.at[at.w], nsend.at[1], nrecv.at[1], width=w).start()
        for j in range(AHEAD):
            across(j, True)
        every[at.w] = on[...]
        for sems in (nsend, nrecv):
            arrived(every.at[: widths - 1], sems.at[1])
        to_partner.start()

    pl.when(c == 0)(lambda: pl.semaphore_wait(ready, 1))
    for j in range(n):

        def pass_on():
            arrived(oq.at[: rows_of([units[k] for k in second_pair(j, n)]), :], arrive.at[j])
            across(j, False)

        some(j < AHEAD, pass_on)
    size = norm.shape[0] // (zeros * widths)
    pl.when(c == 0)(lambda: to_partner.wait_recv())
    for zero in range(zeros):
        for w in range(widths):
            i = zero * widths + w
            flat[:, i * size : (i + 1) * size] = every[w, zero % 2, zero // 2][:, :size]
    norm[...] = flat[0, :].astype(BF16)
    for j in range(BOTH):
        arrived(oq.at[: 2 * rows_of(units[j : j + 1]), :], on_recv.at[j])
        for k in (j, n + j):
            there = region(units[k], diag, rows, 0, c)
            remote(there, there, cross_send, cross_recv, zero=at.partner).start()

    second = rows_of([units[k] for j in range(n) for k in second_pair(j, n)])
    ahead = rows_of([units[k] for j in range(AHEAD) for k in second_pair(j, n)])
    common, early = 2 * rows_of(units[:BOTH]), 2 * rows_of(units[:EARLY])

    @pl.when(c == 0)
    def _():
        arrived(oq.at[:second, :], send)
        arrived(oq.at[:common, :], on_send)

    arrived(oq.at[: second + common, :], cross_send)
    arrived(oq.at[: second + common, :], cross_recv)

    @pl.when(c == 1)
    def _():
        to_partner.wait_send()
        arrived(oq.at[:ahead, :], copied)
        if AHEAD < n:
            arrived(oq.at[: second - ahead, :], send)
        arrived(oq.at[:early, :], on_send)
        arrived(oq.at[: early - common, :], early_recv)


def finish(*refs):
    _, oq, ok, ov, om, dq, dk, dv, dm, rq, rk, rv, rm, ready, copied, on_send, on_recv, send, recv, last_recv = refs
    at = Place()
    c = at.c
    outs, held, diag = (oq, ok, ov, om), (dq, dk, dv, dm), (rq, rk, rv, rm)
    rows = rm.shape[0] // 2
    units = unit_list(rows, om.shape[1], oq.shape[0] // 2, ok.shape[0] // 2)
    n = len(units) // 2
    common, once, whole = (2 * rows_of(units[:count]) for count in (BOTH, n - TWICE, n))
    other_x, other_y = at.xn + at.partner - at.me, at.yn + at.partner - at.me
    enter(at, [], ready, [at.partner, other_x, other_y])

    def onward(j, other=False):
        for k in (j, n + j):
            source = region(units[k], outs, rows, at.chip_x if k < n else at.chip_y, c)
            there = region(units[k], diag, rows, 0, c)
            where = (other_y if k < n else other_x) if other else (at.yn if k < n else at.xn)
            remote(source, there, on_send, last_recv if other else on_recv.at[j], zero=where).start()

    def across(j, early):
        for k in (j, n + j):
            there = region(units[k], diag, rows, 0, c)
            source = region(units[k], held, rows, 0, c) if early else there
            remote(source, there, send, recv, zero=at.partner).start()
            if early:
                pltpu.make_async_copy(source, there, copied).start()

    @pl.when(c == 1)
    def _():
        for j in range(BOTH, n):
            across(j, True)
        arrived(oq.at[: whole - common, :], copied)
        arrived(oq.at[: whole - common, :], send)
        arrived(oq.at[: whole - once, :], last_recv)
        arrived(oq.at[: once - common, :], recv)

    @pl.when(c == 0)
    def _():
        for j in range(BOTH, n):
            onward(j)
        pl.semaphore_wait(ready, 3)
        for j in range(n - TWICE, n):
            onward(j, True)
        for j in range(BOTH, n):
            arrived(oq.at[: 2 * rows_of(units[j : j + 1]), :], on_recv.at[j])
            if j < n - TWICE:
                across(j, False)
        arrived(oq.at[: whole - common + whole - once, :], on_send)
        arrived(oq.at[: once - common, :], send)
        arrived(oq.at[: whole - common, :], recv)


def put_list(rows, sources, p, outs, q, key, second, skip, sem):
    pair = 2 * rows
    there = pl.ds(pl.multiple_of(pair * q, LANES), pair)
    here = there if p is q else pl.ds(pair * p, pair)
    om, oq = outs[3], outs[0]
    half, nq = om.shape[1] // 2, oq.shape[0] // 2
    places = [(3, slice(second * half + skip, (second + 1) * half)), (key, slice(None))]
    places += [(0, slice(c * nq + second * nq // 2, c * nq + (second + 1) * nq // 2)) for c in range(CORES)]
    for a, cut in places:
        src = sources[a].at[here, cut] if a == 3 else sources[a].at[cut, here]
        dst = outs[a].at[there, cut] if a == 3 else outs[a].at[cut, there]
        pltpu.make_async_copy(src, dst, sem).start()


def publish_first(rows, *refs):
    at = Place()
    sources, outs, (token, done) = refs[:4], refs[4:8], refs[8:]
    token[...] = jnp.zeros_like(token)
    pair = 2 * rows
    oq, ok, _, om = sources
    units = unit_list(rows, om.shape[1], oq.shape[0] // 2, ok.shape[0] // 2)
    first = units[0][2]
    for key, second in ((1, 0), (2, 1)):
        put_list(rows, sources, at.chip, outs, at.chip, key, second, 0, done.at[0])
    put_list(rows, sources, at.chip_x, outs, at.chip_x, 1, 0, 0, done.at[1])
    put_list(rows, sources, at.chip_y, outs, at.chip_y, 2, 1, 0, done.at[1])
    block = pl.ds(pl.multiple_of(pair * at.chip_y, LANES), pair)
    pltpu.make_async_copy(om.at[block, :first], outs[3].at[block, :first], done.at[1]).start()
    lists = rows_of(units[: len(units) // 2])
    arrived(oq.at[: 4 * lists, :], done.at[0])
    arrived(oq.at[: 4 * lists + 2 * rows_of(units[:1]), :], done.at[1])


def publish_next(rows, *refs):
    at = Place()
    from_x, from_y, diag, norm = refs[:4], refs[4:8], refs[8:12], refs[12]
    *outs, norm_out, token, done = refs[17:]
    token[...] = jnp.zeros_like(token)
    oq, ok, _, om = outs
    units = unit_list(rows, om.shape[1], oq.shape[0] // 2, ok.shape[0] // 2)
    n = len(units) // 2
    put_list(rows, from_x, 0, outs, at.chip_x, 2, 1, 0, done.at[0])
    put_list(rows, from_y, 0, outs, at.chip_y, 1, 0, units[0][2], done.at[0])
    for j in range(BOTH):
        put_pair(units, j, rows, diag, outs, at.chip_d, done.at[1])
    pltpu.make_async_copy(norm, norm_out, done.at[2]).start()
    arrived(oq.at[: 4 * rows_of(units[:n]) - 2 * rows_of(units[:1]), :], done.at[0])
    arrived(oq.at[: 4 * rows_of(units[:BOTH]), :], done.at[1])
    arrived(norm, done.at[2])


def put_pair(units, j, rows, sources, outs, q, sem):
    for k in (j, len(units) // 2 + j):
        for core in range(CORES):
            src, dst = region(units[k], sources, rows, 0, core), region(units[k], outs, rows, q, core)
            pltpu.make_async_copy(src, dst, sem).start()


def publish_last(rows, *refs):
    at = Place()
    sources, outs, done = refs[:4], refs[8:12], refs[12]
    oq, ok, _, om = outs
    units = unit_list(rows, om.shape[1], oq.shape[0] // 2, ok.shape[0] // 2)
    n = len(units) // 2
    for j in range(BOTH, n):
        put_pair(units, j, rows, sources, outs, at.chip_d, done)
    arrived(oq.at[: 4 * rows_of(units[BOTH:n]), :], done)


def fast_body(zeros, widths, *args):
    tq, lq, hq, tk, lk, hk, tv, lv, hv, tm, lm, hm, nt, ns = args
    rows, depth = tq.shape[0], tq.shape[0] * zeros
    new = jax.ShapeDtypeStruct
    shapes = [(tq.shape[1], depth), (tk.shape[1], depth), (tv.shape[1], depth), (depth, tm.shape[0])]
    pair = 2 * rows
    held = 2 * sum(a * b for a, b in shapes)
    dma = pltpu.SemaphoreType.DMA
    count = len(unit_list(rows, tm.shape[0], tq.shape[1] // 2, tk.shape[1] // 2))
    moved = [tq, lq.T, hq, tk, lk.T, hk, tv, lv.T, hv, tm.T, lm.T, hm, nt[None, :], ns[None, :]]
    rank, mix = hm.shape[0], tm.shape[0]
    halves = (tq.shape[1] + tk.shape[1] + tv.shape[1]) // 2
    norms = (CORES, zeros // CORES, 1, LANES)
    in_vmem, in_hbm = pl.BlockSpec(memory_space=VMEM), pl.BlockSpec(memory_space=HBM)
    *most, on = pl.pallas_call(
        functools.partial(gather, zeros, widths),
        out_shape=[VMEM(s, BF16) for s in shapes] + [VMEM(norms, F32)],
        in_specs=[in_hbm] * len(args),
        out_specs=[in_vmem] * (len(shapes) + 1),
        scratch_shapes=[
            VMEM((rows, mix), BF16), VMEM((rank, mix + rows), BF16), VMEM((pair, halves), BF16),
            VMEM((3, 2, rank, rows), BF16), VMEM((rank, 2 * halves), BF16), VMEM((2, 1, nt.shape[0]), F32),
            VMEM((tq.shape[1] // 2, pair), BF16), VMEM((tk.shape[1] // 2, pair), BF16), VMEM((tv.shape[1] // 2, pair), BF16),
            VMEM((rows, mix), BF16), VMEM((rank, pair), BF16),
            dma((7,)), dma, dma((2,)), dma((2,)), dma, dma((count // 2 + 1,)), dma, dma, dma, dma, dma((3,)), dma((3,)),
        ],
        compiler_params=pltpu.CompilerParams(
            collective_id=0, has_side_effects=True, vmem_limit_bytes=VMEM_BYTES - held - 64 * 1024
        ),
        name="gather_merged",
    )(*moved)
    results = [new(s, BF16) for s in shapes]
    token = VMEM((8, LANES), F32)
    *done, went = pl.pallas_call(
        functools.partial(publish_first, rows),
        out_shape=results + [token],
        in_specs=[in_vmem] * 4,
        out_specs=[in_hbm] * 4 + [in_vmem],
        scratch_shapes=[dma((2,))],
        compiler_params=pltpu.CompilerParams(vmem_limit_bytes=2**20),
        name="publish_first",
    )(*most)
    part = [VMEM((s[0], pair), BF16) for s in shapes[:3]] + [VMEM((pair, shapes[3][1]), BF16)]
    *more, norm = pl.pallas_call(
        functools.partial(spread, zeros, widths),
        out_shape=part * 3 + [VMEM((depth,), BF16)],
        in_specs=[in_vmem] * 6,
        out_specs=[in_vmem] * 13,
        scratch_shapes=[
            VMEM((widths, *norms), F32), VMEM((1, depth), F32),
            pltpu.SemaphoreType.REGULAR, dma, dma, dma((count // 2,)), dma, dma((BOTH,)), dma, dma, dma, dma((2,)), dma((2,)),
        ],
        compiler_params=pltpu.CompilerParams(collective_id=1, has_side_effects=True, vmem_limit_bytes=2**20),
        name="spread",
    )(went, *most, on)
    *done, gain, went = pl.pallas_call(
        functools.partial(publish_next, rows),
        out_shape=results + [new((depth,), BF16), token],
        in_specs=[in_vmem] * 13 + [in_hbm] * 4,
        out_specs=[in_hbm] * 5 + [in_vmem],
        input_output_aliases={13 + k: k for k in range(4)},
        scratch_shapes=[dma((3,))],
        compiler_params=pltpu.CompilerParams(vmem_limit_bytes=2**20),
        name="publish_next",
    )(*more, norm, *done)
    rest = pl.pallas_call(
        finish,
        out_shape=part,
        in_specs=[in_vmem] * 9,
        out_specs=[in_vmem] * 4,
        scratch_shapes=[pltpu.SemaphoreType.REGULAR, dma, dma, dma((count // 2,)), dma, dma, dma],
        compiler_params=pltpu.CompilerParams(collective_id=2, has_side_effects=True, vmem_limit_bytes=2**20),
        name="finish",
    )(went, *most, *more[8:])
    full = pl.pallas_call(
        functools.partial(publish_last, rows),
        out_shape=results,
        in_specs=[in_vmem] * 4 + [in_hbm] * 4,
        out_specs=[in_hbm] * 4,
        input_output_aliases={4 + k: k for k in range(4)},
        scratch_shapes=[dma],
        compiler_params=pltpu.CompilerParams(vmem_limit_bytes=2**20),
        name="publish_last",
    )(*rest, *done)
    return (*full, gain)


def solution(mesh):
    placed = (
        P("zero", "width"), P("zero", None), P(None, "width"),
        P("zero", "width"), P("zero", None), P(None, "width"),
        P("zero", "width"), P("zero", None), P(None, "width"),
        P("width", "zero"), P("width", None), P(None, "zero"),
        P(("zero", "width")), P(("zero", "width")),
    )
    zeros, widths = mesh.shape["zero"], mesh.shape["width"]
    side = math.isqrt(zeros // CORES)

    def body(*args):
        rows, nq, nk, mix = args[0].shape[0], args[0].shape[1] // 2, args[3].shape[1] // 2, args[9].shape[0]
        square = side == 2 and CORES * side * side == zeros and args[6].shape == args[3].shape
        even = (2 * nq + 4 * nk) % mix == 0 and rows % 64 == 0
        if square and even and nq % 128 == 0 and nk % 128 == 0 and mix % (8 * LANES) == 0:
            return fast_body(zeros, widths, *args)
        return plain_body(*args)

    return jax.shard_map(
        body,
        mesh=mesh,
        in_specs=placed,
        out_specs=(P("width", None), P("width", None), P("width", None), P(None, "width"), P()),
        check_vma=False,
    )
```

time: 97.5 us -> 96.6 us (level)
  Pallas kernels: 96.7 us -> 95.7 us
    pallas_call x1, Pallas kernels: 69.1 us -> 39.3 us  [fast_body(): pl.pallas_call(functools.partial(gather, zeros, widths), out_shape=[VMEM(...]
    pallas_call x3 -> x5, Pallas kernels: 27.6 us -> 56.4 us  [the longest x1 33.1 us: fast_body(): pl.pallas_call(functools.partial(spread, zeros, widths), out_shape=part *...]
where the time goes in v3:
time: 96.6 us; the launch traced here: 96.4 us
  Pallas kernels  95.7 us (99%)
    pallas_call x1, Pallas kernels, fast_body(): pl.pallas_call(functools.partial(gather, zeros, widths), out_shape=[VMEM(...  39.3 us
    pallas_call x1, Pallas kernels, fast_body(): pl.pallas_call(functools.partial(spread, zeros, widths), out_shape=part *...  33.1 us
    pallas_call x1, Pallas kernels, fast_body(): pl.pallas_call(finish, out_shape=part, in_specs=[in_vmem] * 9, out_specs=...  14.4 us
    pallas_call x1, Pallas kernels, fast_body(): pl.pallas_call(functools.partial(publish_first, rows), out_shape=results...  4.16 us
    pallas_call x1, Pallas kernels, fast_body(): pl.pallas_call(functools.partial(publish_next, rows), out_shape=results +...  2.92 us

profile of v3, /device:TPU:0, one launch (start us, length us, event | category | flops | bytes accessed | tf_op | source)
XLA Modules:
  0.0 96.4 jit_solution(4314310570812778183)
XLA Ops:
  0.6 39.3 %gather_merged.1 = (bf16[1024,3584]{1,0:T(8,128)(2,1)S(1)}, bf16[512,3584]{1,0:T(8,128)(2,1)S(1)}, bf16[512,3584]{1,0:T(8,128)(2,1)S(1)}, bf16[3584,1024]{1,0:T(8,128)(2,1)S(1)}, f32[2,4,1,128]{3,2,1,0:T(1,128)S(1)}) custom-call(bf16[448,1024]{1,0:T(8,128)(2,1)} %tq_h.1, bf16[32,448]{1,0:T(8,128)(2,1)} %bitcast.9, bf16[32,1024]{1,0:T(8,128)(2,1)} %hq_h.1, ...), custom_call_target="tpu_custom_call" | custom-call | tf_op jit(solution)/shard_map/gather_merged/pallas_call | solution.py:527
  40.0 4.2 %publish_first.1 = (bf16[1024,3584]{1,0:T(8,128)(2,1)}, bf16[512,3584]{1,0:T(8,128)(2,1)}, bf16[512,3584]{1,0:T(8,128)(2,1)}, bf16[3584,1024]{1,0:T(8,128)(2,1)}, f32[8,128]{1,0:T(8,128)S(1)}) custom-call(bf16[1024,3584]{1,0:T(8,128)(2,1)S(1)} %get-tuple-element.42.refs_0_.refs_1_, bf16[512,3584]{1,0:T(8,128)(2,1)S(1)} %get-tuple-element.43.refs_1_.refs_2_, ...), custom_call_target="tpu_custom_call" | custom-call | tf_op jit(solution)/shard_map/publish_first/pallas_call | solution.py:546
  44.1 33.1 %spread.1 = (bf16[1024,896]{1,0:T(8,128)(2,1)S(1)}, bf16[512,896]{1,0:T(8,128)(2,1)S(1)}, bf16[512,896]{1,0:T(8,128)(2,1)S(1)}, bf16[896,1024]{1,0:T(8,128)(2,1)...) custom-call(f32[8,128]{1,0:T(8,128)S(1)} %get-tuple-element.46.refs_, ...), custom_call_target="tpu_custom_call" | custom-call | tf_op jit(solution)/shard_map/spread/pallas_call | solution.py:556
  77.2 2.9 %publish_next.1 = (bf16[1024,3584]{1,0:T(8,128)(2,1)}, bf16[512,3584]{1,0:T(8,128)(2,1)}, bf16[512,3584]{1,0:T(8,128)(2,1)}, bf16[3584,1024]{1,0:T(8,128)(2,1)},...) custom-call(bf16[1024,896]{1,0:T(8,128)(2,1)S(1)} %get-tuple-element, ...), custom_call_target="tpu_custom_call", output_to_operand_aliasing={{0}: (13, {}), {1}: (14, {}), {2}: (15, {}), {3}: (16, {})} | custom-call | tf_op jit(solution)/shard_map/publish_next/pallas_call | solution.py:568
  80.1 14.4 %finish.1 = (bf16[1024,896]{1,0:T(8,128)(2,1)S(1)}, bf16[512,896]{1,0:T(8,128)(2,1)S(1)}, bf16[512,896]{1,0:T(8,128)(2,1)S(1)}, bf16[896,1024]{1,0:T(8,128)(2,1)S(1)}) custom-call(f32[8,128]{1,0:T(8,128)S(1)} %get-tuple-element.65.refs_0_, bf16[1024,3584]{1,0:T(8,128)(2,1)S(1)} %get-tuple-element.42.refs_0_.refs_1_, ...), custom_call_target="tpu_custom_call" | custom-call | tf_op jit(solution)/shard_map/finish/pallas_call | solution.py:578
  94.6 1.8 %publish_last.1 = (bf16[1024,3584]{1,0:T(8,128)(2,1)}, bf16[512,3584]{1,0:T(8,128)(2,1)}, bf16[512,3584]{1,0:T(8,128)(2,1)}, bf16[3584,1024]{1,0:T(8,128)(2,1)}) custom-call(bf16[1024,896]{1,0:T(8,128)(2,1)S(1)} %get-tuple-element.66.refs_0_, ...), custom_call_target="tpu_custom_call", output_to_operand_aliasing={{0}: (4, {}), {1}: (5, {}), {2}: (6, {}), {3}: (7, {})} | custom-call | tf_op jit(solution)/shard_map/publish_last/pallas_call | solution.py:587

commit v4 on v3

--- a/solution.py
+++ b/solution.py
@@ -14,7 +14,7 @@
 F32 = jnp.float32
 BF16 = jnp.bfloat16
 AHEAD = 8
-BOTH = 3
+BOTH = 4
 EARLY = 9
 TWICE = 1
 VMEM_BYTES = 67_043_328
@@ -63,7 +63,7 @@
 def unit_list(rows, mix, nq, nk):
     eighth = mix // 8
     mixed = ((0, eighth), (eighth, 2 * eighth), (3 * eighth, eighth))
-    query = ((0, nq // 4), (nq // 4, nq // 4))
+    query = ((0, nq // 8), (nq // 8, 3 * nq // 8))
     parts = ((0, nk // 2), (nk // 2, nk // 4), (3 * nk // 4, nk // 8), (7 * nk // 8, nk // 8))
     return [
         (a, at + half, size)
@@ -113,12 +113,13 @@
     def fetch(src, dst, sem):
         pltpu.make_async_copy(src, dst, fetched.at[sem]).start()
 
+    barrier = pltpu.get_barrier_semaphore()
+    for other in (at.xn, at.yn, at.partner):
+        tell(barrier, zero=other)
+
+    fetch(tm_h.at[:, :first], tm.at[:, :first], FIRST)
+    fetch(hm_h, pair_m.at[:, mix:], LOW_HIGH)
     fetch(lm_h, pair_m.at[:, :mix], LOW_HIGH)
-    fetch(hm_h, pair_m.at[:, mix:], LOW_HIGH)
-    fetch(tm_h.at[:, :first], tm.at[:, :first], FIRST)
-    barrier = pltpu.get_barrier_semaphore()
-    for other in (at.partner, at.xn, at.yn):
-        tell(barrier, zero=other)
     fetch(nt_h, gains.at[0], GAINS)
     fetch(ns_h, gains.at[1], GAINS)
     fetch(tm_h.at[:, first:], tm.at[:, first:], OTHERS)
@@ -327,16 +328,17 @@
     def some(core_0_alone, step):
         pl.when(c == 0)(step) if core_0_alone else step()
 
-    for j in range(n):
-        some(j < AHEAD, lambda: own(j))
-    for j in range(BOTH):
-        onward(j)
+    def send_all(first, pairs):
+        for j in range(first, n):
+            own(j)
+        for j in range(pairs):
+            onward(j)
+
+    pl.when(c == 0)(lambda: send_all(0, BOTH))
     to_partner = remote(every, every, nsend.at[0], nrecv.at[0], zero=at.partner)
 
     @pl.when(c == 1)
     def _():
-        for j in range(BOTH, EARLY):
-            onward(j)
         for w in z_peers:
             remote(on, every.at[at.w], nsend.at[1], nrecv.at[1], width=w).start()
         for j in range(AHEAD):
@@ -344,6 +346,7 @@
         every[at.w] = on[...]
         for sems in (nsend, nrecv):
             arrived(every.at[: widths - 1], sems.at[1])
+        send_all(AHEAD, EARLY)
         to_partner.start()
 
     pl.when(c == 0)(lambda: pl.semaphore_wait(ready, 1))
@@ -406,7 +409,7 @@
             source = region(units[k], outs, rows, at.chip_x if k < n else at.chip_y, c)
             there = region(units[k], diag, rows, 0, c)
             where = (other_y if k < n else other_x) if other else (at.yn if k < n else at.xn)
-            remote(source, there, on_send, last_recv if other else on_recv.at[j], zero=where).start()
+            remote(source, there, on_send, last_recv if other else on_recv.at[j - BOTH], zero=where).start()
 
     def across(j, early):
         for k in (j, n + j):
@@ -433,7 +436,7 @@
         for j in range(n - TWICE, n):
             onward(j, True)
         for j in range(BOTH, n):
-            arrived(oq.at[: 2 * rows_of(units[j : j + 1]), :], on_recv.at[j])
+            arrived(oq.at[: 2 * rows_of(units[j : j + 1]), :], on_recv.at[j - BOTH])
             if j < n - TWICE:
                 across(j, False)
         arrived(oq.at[: whole - common + whole - once, :], on_send)
@@ -580,7 +583,7 @@
         out_shape=part,
         in_specs=[in_vmem] * 9,
         out_specs=[in_vmem] * 4,
-        scratch_shapes=[pltpu.SemaphoreType.REGULAR, dma, dma, dma((count // 2,)), dma, dma, dma],
+        scratch_shapes=[pltpu.SemaphoreType.REGULAR, dma, dma, dma((count // 2 - BOTH,)), dma, dma, dma],
         compiler_params=pltpu.CompilerParams(collective_id=2, has_side_effects=True, vmem_limit_bytes=2**20),
         name="finish",
     )(went, *most, *more[8:])

time: 96.6 us -> 96.4 us (level)
  no operation moved by 1% of the time
where the time goes in v4:
time: 96.4 us; the launch traced here: 96.2 us
  Pallas kernels  95.5 us (99%)
    pallas_call x1, Pallas kernels, fast_body(): pl.pallas_call(functools.partial(gather, zeros, widths), out_shape=[VMEM(...  39.3 us
    pallas_call x1, Pallas kernels, fast_body(): pl.pallas_call(functools.partial(spread, zeros, widths), out_shape=part *...  33.8 us
    pallas_call x1, Pallas kernels, fast_body(): pl.pallas_call(finish, out_shape=part, in_specs=[in_vmem] * 9, out_specs=...  13.6 us
    pallas_call x1, Pallas kernels, fast_body(): pl.pallas_call(functools.partial(publish_first, rows), out_shape=results...  4.16 us
    pallas_call x1, Pallas kernels, fast_body(): pl.pallas_call(functools.partial(publish_next, rows), out_shape=results +...  3.06 us

profile of v4, /device:TPU:0, one launch (start us, length us, event | category | flops | bytes accessed | tf_op | source)
XLA Modules:
  0.0 96.2 jit_solution(13670306299313303970)
XLA Ops:
  0.6 39.3 %gather_merged.1 = (bf16[1024,3584]{1,0:T(8,128)(2,1)S(1)}, bf16[512,3584]{1,0:T(8,128)(2,1)S(1)}, bf16[512,3584]{1,0:T(8,128)(2,1)S(1)}, bf16[3584,1024]{1,0:T(8,128)(2,1)S(1)}, f32[2,4,1,128]{3,2,1,0:T(1,128)S(1)}) custom-call(bf16[448,1024]{1,0:T(8,128)(2,1)} %tq_h.1, bf16[32,448]{1,0:T(8,128)(2,1)} %bitcast.9, bf16[32,1024]{1,0:T(8,128)(2,1)} %hq_h.1, ...), custom_call_target="tpu_custom_call" | custom-call | tf_op jit(solution)/shard_map/gather_merged/pallas_call | solution.py:530
  40.0 4.2 %publish_first.1 = (bf16[1024,3584]{1,0:T(8,128)(2,1)}, bf16[512,3584]{1,0:T(8,128)(2,1)}, bf16[512,3584]{1,0:T(8,128)(2,1)}, bf16[3584,1024]{1,0:T(8,128)(2,1)}, f32[8,128]{1,0:T(8,128)S(1)}) custom-call(bf16[1024,3584]{1,0:T(8,128)(2,1)S(1)} %get-tuple-element.42.refs_0_.refs_1_, bf16[512,3584]{1,0:T(8,128)(2,1)S(1)} %get-tuple-element.43.refs_1_.refs_2_, ...), custom_call_target="tpu_custom_call" | custom-call | tf_op jit(solution)/shard_map/publish_first/pallas_call | solution.py:549
  44.1 33.8 %spread.1 = (bf16[1024,896]{1,0:T(8,128)(2,1)S(1)}, bf16[512,896]{1,0:T(8,128)(2,1)S(1)}, bf16[512,896]{1,0:T(8,128)(2,1)S(1)}, bf16[896,1024]{1,0:T(8,128)(2,1)...) custom-call(f32[8,128]{1,0:T(8,128)S(1)} %get-tuple-element.46.refs_, ...), custom_call_target="tpu_custom_call" | custom-call | tf_op jit(solution)/shard_map/spread/pallas_call | solution.py:559
  77.9 3.1 %publish_next.1 = (bf16[1024,3584]{1,0:T(8,128)(2,1)}, bf16[512,3584]{1,0:T(8,128)(2,1)}, bf16[512,3584]{1,0:T(8,128)(2,1)}, bf16[3584,1024]{1,0:T(8,128)(2,1)},...) custom-call(bf16[1024,896]{1,0:T(8,128)(2,1)S(1)} %get-tuple-element, ...), custom_call_target="tpu_custom_call", output_to_operand_aliasing={{0}: (13, {}), {1}: (14, {}), {2}: (15, {}), {3}: (16, {})} | custom-call | tf_op jit(solution)/shard_map/publish_next/pallas_call | solution.py:571
  81.0 13.6 %finish.1 = (bf16[1024,896]{1,0:T(8,128)(2,1)S(1)}, bf16[512,896]{1,0:T(8,128)(2,1)S(1)}, bf16[512,896]{1,0:T(8,128)(2,1)S(1)}, bf16[896,1024]{1,0:T(8,128)(2,1)S(1)}) custom-call(f32[8,128]{1,0:T(8,128)S(1)} %get-tuple-element.65.refs_0_, bf16[1024,3584]{1,0:T(8,128)(2,1)S(1)} %get-tuple-element.42.refs_0_.refs_1_, ...), custom_call_target="tpu_custom_call" | custom-call | tf_op jit(solution)/shard_map/finish/pallas_call | solution.py:581
  94.5 1.7 %publish_last.1 = (bf16[1024,3584]{1,0:T(8,128)(2,1)}, bf16[512,3584]{1,0:T(8,128)(2,1)}, bf16[512,3584]{1,0:T(8,128)(2,1)}, bf16[3584,1024]{1,0:T(8,128)(2,1)}) custom-call(bf16[1024,896]{1,0:T(8,128)(2,1)S(1)} %get-tuple-element.66.refs_0_, ...), custom_call_target="tpu_custom_call", output_to_operand_aliasing={{0}: (4, {}), {1}: (5, {}), {2}: (6, {}), {3}: (7, {})} | custom-call | tf_op jit(solution)/shard_map/publish_last/pallas_call | solution.py:590

commit v5 on v4

--- a/solution.py
+++ b/solution.py
@@ -13,9 +13,9 @@
 LANES = 128
 F32 = jnp.float32
 BF16 = jnp.bfloat16
-AHEAD = 8
+AHEAD = 9
 BOTH = 4
-EARLY = 9
+EARLY = 10
 TWICE = 1
 VMEM_BYTES = 67_043_328
 VMEM = pltpu.VMEM
@@ -63,7 +63,7 @@
 def unit_list(rows, mix, nq, nk):
     eighth = mix // 8
     mixed = ((0, eighth), (eighth, 2 * eighth), (3 * eighth, eighth))
-    query = ((0, nq // 8), (nq // 8, 3 * nq // 8))
+    query = ((0, nq // 8), (nq // 8, nq // 8), (nq // 4, nq // 4))
     parts = ((0, nk // 2), (nk // 2, nk // 4), (3 * nk // 4, nk // 8), (7 * nk // 8, nk // 8))
     return [
         (a, at + half, size)
@@ -219,12 +219,12 @@
     merge(0, oq, own_q)
     small[0].wait()
     small[1].start()
-    for j in (3, 4):
+    for j in (3, 4, 5):
         to_x(j)
         to_y(n + j)
     merge(1, ok, own_k)
     merge(2, ov, own_v)
-    for j in range(5, n):
+    for j in range(6, n):
         to_x(j)
         to_y(n + j)
     @pl.when(c == 1)

time: 96.4 us -> 96.4 us (level)
  no operation moved by 1% of the time
where the time goes in v5:
time: 96.4 us; the launch traced here: 96.2 us
  Pallas kernels  95.6 us (99%)
    pallas_call x1, Pallas kernels, fast_body(): pl.pallas_call(functools.partial(gather, zeros, widths), out_shape=[VMEM(...  39.3 us
    pallas_call x1, Pallas kernels, fast_body(): pl.pallas_call(functools.partial(spread, zeros, widths), out_shape=part *...  33.8 us
    pallas_call x1, Pallas kernels, fast_body(): pl.pallas_call(finish, out_shape=part, in_specs=[in_vmem] * 9, out_specs=...  13.6 us
    pallas_call x1, Pallas kernels, fast_body(): pl.pallas_call(functools.partial(publish_first, rows), out_shape=results...  4.16 us
    pallas_call x1, Pallas kernels, fast_body(): pl.pallas_call(functools.partial(publish_next, rows), out_shape=results +...  3.06 us

profile of v5, /device:TPU:0, one launch (start us, length us, event | category | flops | bytes accessed | tf_op | source)
XLA Modules:
  0.0 96.2 jit_solution(16979609072510919153)
XLA Ops:
  0.6 39.3 %gather_merged.1 = (bf16[1024,3584]{1,0:T(8,128)(2,1)S(1)}, bf16[512,3584]{1,0:T(8,128)(2,1)S(1)}, bf16[512,3584]{1,0:T(8,128)(2,1)S(1)}, bf16[3584,1024]{1,0:T(8,128)(2,1)S(1)}, f32[2,4,1,128]{3,2,1,0:T(1,128)S(1)}) custom-call(bf16[448,1024]{1,0:T(8,128)(2,1)} %tq_h.1, bf16[32,448]{1,0:T(8,128)(2,1)} %bitcast.9, bf16[32,1024]{1,0:T(8,128)(2,1)} %hq_h.1, ...), custom_call_target="tpu_custom_call" | custom-call | tf_op jit(solution)/shard_map/gather_merged/pallas_call | solution.py:530
  40.0 4.2 %publish_first.1 = (bf16[1024,3584]{1,0:T(8,128)(2,1)}, bf16[512,3584]{1,0:T(8,128)(2,1)}, bf16[512,3584]{1,0:T(8,128)(2,1)}, bf16[3584,1024]{1,0:T(8,128)(2,1)}, f32[8,128]{1,0:T(8,128)S(1)}) custom-call(bf16[1024,3584]{1,0:T(8,128)(2,1)S(1)} %get-tuple-element.42.refs_0_.refs_1_, bf16[512,3584]{1,0:T(8,128)(2,1)S(1)} %get-tuple-element.43.refs_1_.refs_2_, ...), custom_call_target="tpu_custom_call" | custom-call | tf_op jit(solution)/shard_map/publish_first/pallas_call | solution.py:549
  44.1 33.8 %spread.1 = (bf16[1024,896]{1,0:T(8,128)(2,1)S(1)}, bf16[512,896]{1,0:T(8,128)(2,1)S(1)}, bf16[512,896]{1,0:T(8,128)(2,1)S(1)}, bf16[896,1024]{1,0:T(8,128)(2,1)...) custom-call(f32[8,128]{1,0:T(8,128)S(1)} %get-tuple-element.46.refs_, ...), custom_call_target="tpu_custom_call" | custom-call | tf_op jit(solution)/shard_map/spread/pallas_call | solution.py:559
  77.9 3.1 %publish_next.1 = (bf16[1024,3584]{1,0:T(8,128)(2,1)}, bf16[512,3584]{1,0:T(8,128)(2,1)}, bf16[512,3584]{1,0:T(8,128)(2,1)}, bf16[3584,1024]{1,0:T(8,128)(2,1)},...) custom-call(bf16[1024,896]{1,0:T(8,128)(2,1)S(1)} %get-tuple-element, ...), custom_call_target="tpu_custom_call", output_to_operand_aliasing={{0}: (13, {}), {1}: (14, {}), {2}: (15, {}), {3}: (16, {})} | custom-call | tf_op jit(solution)/shard_map/publish_next/pallas_call | solution.py:571
  81.0 13.6 %finish.1 = (bf16[1024,896]{1,0:T(8,128)(2,1)S(1)}, bf16[512,896]{1,0:T(8,128)(2,1)S(1)}, bf16[512,896]{1,0:T(8,128)(2,1)S(1)}, bf16[896,1024]{1,0:T(8,128)(2,1)S(1)}) custom-call(f32[8,128]{1,0:T(8,128)S(1)} %get-tuple-element.65.refs_0_, bf16[1024,3584]{1,0:T(8,128)(2,1)S(1)} %get-tuple-element.42.refs_0_.refs_1_, ...), custom_call_target="tpu_custom_call" | custom-call | tf_op jit(solution)/shard_map/finish/pallas_call | solution.py:581
  94.5 1.7 %publish_last.1 = (bf16[1024,3584]{1,0:T(8,128)(2,1)}, bf16[512,3584]{1,0:T(8,128)(2,1)}, bf16[512,3584]{1,0:T(8,128)(2,1)}, bf16[3584,1024]{1,0:T(8,128)(2,1)}) custom-call(bf16[1024,896]{1,0:T(8,128)(2,1)S(1)} %get-tuple-element.66.refs_0_, ...), custom_call_target="tpu_custom_call", output_to_operand_aliasing={{0}: (4, {}), {1}: (5, {}), {2}: (6, {}), {3}: (7, {})} | custom-call | tf_op jit(solution)/shard_map/publish_last/pallas_call | solution.py:590
